TPU v7x, 32 devices: a whole 2x2x4 slice. The times are simulated.
32 devices in a mesh: gx: 8 (over z, y), gy: 4 (over x, core).
Axes of the slice: x: 2, y: 2, z: 4, core: 2. Of those that a mesh axis runs over, the one named last changes fastest.
Arguments:
- charge_density: float32 [256, 256, 256], P('gx', 'gy'), may hold values from -5080 to 5140
Outputs:
- potential: float32 [256, 256, 256], P('gx', 'gy')
- energies: float32 [2], replicated
All inputs are finite; a program needn't handle non-finite values.
Results may differ from a plain program's by a relative error of at most 0.0003.
Values sent between devices are 32-bit elements.
A program may use at most 192 MiB of HBM per device.

v0:
```python
import functools
import math

import jax
import jax.numpy as jnp
import numpy as np
from jax import lax
from jax.experimental import pallas as pl
from jax.experimental.pallas import tpu as pltpu
from jax.sharding import PartitionSpec as P

ORDER = 16
DEG = ORDER + 1
RATIO = 1.1
RADIUS = math.sqrt(3.0) / 2.0
HIGH = lax.Precision.HIGH
BEST = lax.Precision.HIGHEST
LANES = 128
MESH = pl.DeviceIdType.MESH


def solid_harmonics(x, y, z):
    rr = x * x + y * y + z * z
    out = np.zeros((DEG, 2 * DEG - 1) + x.shape)
    cos = np.zeros((DEG, DEG) + x.shape)
    sin = np.zeros((DEG, DEG) + x.shape)
    cos[0, 0] = 1.0
    for l in range(1, DEG):
        s = 1.0 if l == 1 else math.sqrt((2 * l - 1) / (2.0 * l))
        cos[l, l] = s * (x * cos[l - 1, l - 1] - y * sin[l - 1, l - 1])
        sin[l, l] = s * (x * sin[l - 1, l - 1] + y * cos[l - 1, l - 1])
        for m in range(l):
            div = math.sqrt(l * l - m * m)
            far = math.sqrt((l - 1) * (l - 1) - m * m) if l - 1 > m else 0.0
            for f in (cos, sin):
                f[l, m] = (2 * l - 1) * z * f[l - 1, m] / div
                if l >= 2 and far:
                    f[l, m] = f[l, m] - far * rr * f[l - 2, m] / div
    out[:, :DEG] = cos
    out[:, DEG:] = sin[:, 1:]
    return out


def face_tensors():
    t = np.cos(np.pi * (np.arange(DEG) + 0.5) / DEG)
    fwd = np.cos(np.arange(DEG)[:, None] * np.arccos(t)[None, :]) * (2.0 / DEG)
    fwd[0] *= 0.5
    u, v = np.meshgrid(t / 2, t / 2, indexing="ij")
    half = np.full_like(u, 0.5)
    tensors = []
    for pts in ((half, u, v), (u, half, v), (u, v, half)):
        vals = solid_harmonics(*pts)
        tensors.append(np.einsum("pu,lfuv,qv->lfpq", fwd, vals, fwd))
    par = np.ones((3, DEG, 2 * DEG - 1))
    for l in range(DEG):
        for f in range(2 * DEG - 1):
            m, odd = (f, 0) if f < DEG else (f - ORDER, 1)
            par[0, l, f] = (-1.0) ** (m + odd)
            par[1, l, f] = (-1.0) ** odd
            par[2, l, f] = (-1.0) ** (l + m)
    return np.stack(tensors).astype(np.float32).reshape(3, DEG, 2 * DEG - 1, DEG * DEG), par.astype(np.float32)


def expansion_weights():
    w = np.zeros((DEG, 2 * DEG - 1))
    for l in range(DEG):
        for f in range(2 * DEG - 1):
            m = f if f < DEG else f - ORDER
            w[l, f] = (1.0 if m == 0 else 2.0) / (4.0 * math.pi * RADIUS * RATIO ** (l + 1))
    return w.astype(np.float32)


def split(x):
    hi = x.astype(jnp.bfloat16)
    return hi, (x - hi.astype(jnp.float32)).astype(jnp.bfloat16)


def dot(a, b):
    return jnp.dot(a, b, preferred_element_type=jnp.float32)


def left_mul(mat, x):
    hi, lo = split(x)
    return dot(mat[0], hi) + dot(mat[0], lo) + dot(mat[1], hi)


def right_mul(x, mat):
    hi, lo = split(x)
    return dot(hi, mat[0]) + dot(lo, mat[0]) + dot(hi, mat[1])


def split_table(table):
    t = jnp.asarray(np.asarray(table, np.float32))
    return jnp.stack(split(t))


def turn(x, shift):
    width = x.shape[-1]
    shift %= width
    return pltpu.roll(x, shift, x.ndim - 1) if shift else x


class Plan:
    def __init__(self, ca, cb, n, gx, gy):
        self.ca, self.cb, self.n, self.gx, self.gy = ca, cb, n, gx, gy
        self.kb = n // gy
        self.jb = n // gx
        self.width = LANES
        self.pack = LANES // self.kb
        self.sub = ca // self.pack
        self.step = max(1, self.sub // 8)
        self.pair = 2 if self.step % 2 == 0 else 1
        self.chunks = self.sub // self.step
        self.tile = min(n, 64)

    def lanes(self, rows):
        return lax.broadcasted_iota(jnp.int32, (rows, LANES), 1) // self.kb


def greet(p):
    ix, iy = lax.axis_index("gx"), lax.axis_index("gy")
    barrier = pltpu.get_barrier_semaphore()
    for d in range(1, p.gx):
        pl.semaphore_signal(barrier, inc=1, device_id={"gx": lax.rem(ix + d, p.gx)}, device_id_type=MESH)
    for d in range(1, p.gy):
        pl.semaphore_signal(barrier, inc=1, device_id={"gy": lax.rem(iy + d, p.gy)}, device_id_type=MESH)
    pl.semaphore_wait(barrier, p.gx + p.gy - 2)


def remote(src, dst, send, recv, where):
    return pltpu.make_async_remote_copy(
        src_ref=src, dst_ref=dst, send_sem=send, recv_sem=recv, device_id=where, device_id_type=MESH
    )


def mode_tables(p, epsj_ref, epsk_ref, tab_ref):
    iy = lax.axis_index("gy")
    sigma = epsj_ref[...] + epsk_ref[iy][0:1]
    s = 0.5 * jnp.sqrt(sigma)
    t = jnp.sqrt(1.0 + s * s)
    theta = 2.0 * jnp.log1p(s + s * s / (1.0 + t))
    lam = jnp.exp(-theta)
    tab_ref[0] = lam
    tab_ref[1] = 1.0 / (4.0 * s * t)
    tab_ref[2] = jnp.exp(-theta * float(p.sub))
    tab_ref[3] = jnp.exp(-theta * float(p.ca))
    tab_ref[4] = lam / (1.0 - jnp.exp(-theta * (2.0 * (p.n + 1))))
    tab_ref[5] = jnp.exp(-theta * float(p.n + 1))


def edge_sums(p, v_ref, tab_ref, left_ref, right_ref, edge_ref):
    for t in range(p.n // p.tile):
        rows = pl.ds(t * p.tile, p.tile)
        lam, lsub = tab_ref[0, rows], tab_ref[2, rows]
        left, right = v_ref[0, rows], v_ref[p.sub - 1, rows]
        for i in range(1, p.sub):
            left = left * lam + v_ref[i, rows]
            right = right * lam + v_ref[p.sub - 1 - i, rows]
        left_ref[rows] = left
        right_ref[rows] = right
        dev_l, dev_r = left, right
        for g in range(1, p.pack):
            dev_l = dev_l * lsub + turn(left, -g * p.kb)
            dev_r = dev_r * lsub + turn(right, g * p.kb)
        edge_ref[rows] = jnp.where(p.lanes(p.tile) == 0, dev_l, dev_r)


def line_exchange(p, tab_ref, edge_ref, got_ref, back_ref, ends_ref, sems, between):
    ix = lax.axis_index("gx")
    mine = pl.ds(ix * p.jb, p.jb)

    def copies(src, dst, base):
        out = []
        for d in range(1, p.gx):
            r = lax.rem(ix + d, p.gx)
            out.append(remote(src(r), dst, sems.at[base, d], sems.at[base + 1, d], {"gx": r}))
        return out

    first = copies(lambda r: edge_ref.at[pl.ds(r * p.jb, p.jb)], got_ref.at[ix], 0)
    for c in first:
        c.start()
    got_ref[ix] = edge_ref[mine]
    between(0)
    for c in first:
        c.wait_recv()
    lower = p.lanes(p.jb) == 0
    blk, det, lnp = tab_ref[3, mine], tab_ref[4, mine], tab_ref[5, mine]
    state = jnp.zeros((p.jb, LANES), jnp.float32)
    states = []
    for t in range(p.gx):
        states.append(state)
        state = state * blk + jnp.where(lower, got_ref[t], got_ref[p.gx - 1 - t])
    other = jnp.where(lower, turn(state, p.kb), turn(state, -p.kb))
    image = (other - state * lnp) * det
    for t in range(p.gx):
        states[t] = states[t] - image
        image = image * blk
    for t in range(p.gx):
        back_ref[t] = jnp.where(lower, states[t], states[p.gx - 1 - t])
    second = copies(lambda r: back_ref.at[r], ends_ref.at[mine], 2)
    for c in second:
        c.start()
    ends_ref[mine] = back_ref[ix]
    between(1)
    for c in second:
        c.wait_recv()
    for c in first + second:
        c.wait_send()


def carries(p, rows, tab_ref, left_ref, right_ref, ends_ref):
    lsub = tab_ref[2, rows]
    left, right = left_ref[rows], right_ref[rows]
    a = b = ends_ref[rows]
    place = p.lanes(p.tile)
    for g in range(p.pack - 1):
        a = jnp.where(place == g + 1, turn(a * lsub + left, p.kb), a)
        h = p.pack - 1 - g
        b = jnp.where(place == h - 1, turn(b * lsub + right, -p.kb), b)
    return a, b


def forward_kernel(p, rho_ref, sz_ref, sy_ref, epsj_ref, epsk_ref, rhs_ref, first_ref, tab_ref,
                   x_ref, send_ref, spec_ref, left_ref, right_ref, edge_ref, got_ref, back_ref, ends_ref,
                   in_sems, out_sems, land_sems, line_sems):
    iy = lax.axis_index("gy")

    def load(c, g):
        rows = pl.ds(g * p.sub + c * p.step, p.step)
        return pltpu.make_async_copy(rho_ref.at[rows], x_ref.at[rows], in_sems.at[c, g])

    for c in range(p.chunks):
        for g in range(p.pack):
            load(c, g).start()
    greet(p)

    def swap(c, d):
        q = lax.rem(iy + d, p.gy)
        planes = pl.ds(c * p.step, p.step)
        return remote(send_ref.at[q, planes], spec_ref.at[planes, pl.ds(iy * p.cb, p.cb)],
                      out_sems.at[c, d], land_sems.at[c, d], {"gy": q})

    block = p.step * p.cb
    order = list(range(p.gy // 2, p.gy)) + list(range(1, p.gy // 2))

    def transform(c, carry):
        for g in range(p.pack):
            load(c, g).wait()
        x = jnp.concatenate(
            [x_ref[pl.ds(g * p.sub + c * p.step, p.step)].reshape(block, p.n) for g in range(p.pack)], axis=0
        )
        y = right_mul(x, sz_ref)
        place = p.lanes(block)
        planes = pl.ds(c * p.step, p.step)
        for q in range(p.gy):
            col, off = divmod(q * p.kb, LANES)
            piece = None
            for g in range(p.pack):
                part = turn(y[g * block:(g + 1) * block, col * LANES:(col + 1) * LANES], g * p.kb - off)
                piece = part if piece is None else jnp.where(place == g, part, piece)
            send_ref[q, planes] = piece.reshape(p.step, p.cb, LANES)

        @pl.when(c > 0)
        def _():
            for d in order:
                swap(c - 1, d).start()

        spec_ref[planes, pl.ds(iy * p.cb, p.cb)] = send_ref[iy, planes]
        return carry

    lax.fori_loop(0, p.chunks, transform, 0)
    mode_tables(p, epsj_ref, epsk_ref, tab_ref)
    for d in order:
        swap(p.chunks - 1, d).start()

    def across(c, carry):
        for d in order:
            swap(c, d).wait_recv()
        for i in range(0, p.step, p.pair):
            s = c * p.step + i
            x = jnp.concatenate([spec_ref[s + e] for e in range(p.pair)], axis=1)
            y = left_mul(sy_ref, x)
            for e in range(p.pair):
                rhs_ref[s + e] = y[:, e * LANES:(e + 1) * LANES]
        return carry

    lax.fori_loop(0, p.chunks, across, 0)
    edge_sums(p, rhs_ref, tab_ref, left_ref, right_ref, edge_ref)
    line_exchange(p, tab_ref, edge_ref, got_ref, back_ref, ends_ref, line_sems, lambda stage: None)

    for t in range(p.n // p.tile):
        rows = pl.ds(t * p.tile, p.tile)
        lam, inv = tab_ref[0, rows], tab_ref[1, rows]
        a, b = carries(p, rows, tab_ref, left_ref, right_ref, ends_ref)
        for i in range(p.sub - 1, -1, -1):
            b = b * lam
            first_ref[i, rows] = b
            b = b + rhs_ref[i, rows]
        for i in range(p.sub):
            a = a * lam + rhs_ref[i, rows]
            first_ref[i, rows] = (a + first_ref[i, rows]) * inv

    def drain(c, carry):
        for d in order:
            swap(c, d).wait_send()
        return carry

    lax.fori_loop(0, p.chunks, drain, 0)


def forward(p, rho, sz, sy, epsj, epsk):
    f32 = jnp.float32
    cube = (p.sub, p.n, LANES)
    vmem = pl.BlockSpec(memory_space=pltpu.VMEM)
    dma = pltpu.SemaphoreType.DMA
    return pl.pallas_call(
        functools.partial(forward_kernel, p),
        in_specs=[pl.BlockSpec(memory_space=pl.ANY)] + [vmem] * 4,
        out_specs=[vmem] * 3,
        out_shape=[
            jax.ShapeDtypeStruct(cube, f32),
            jax.ShapeDtypeStruct(cube, f32),
            jax.ShapeDtypeStruct((6, p.n, LANES), f32),
        ],
        scratch_shapes=[
            pltpu.VMEM((p.ca, p.cb, p.n), f32),
            pltpu.VMEM((p.gy, p.sub, p.cb, LANES), f32),
            pltpu.VMEM(cube, f32),
            pltpu.VMEM((p.n, LANES), f32),
            pltpu.VMEM((p.n, LANES), f32),
            pltpu.VMEM((p.n, LANES), f32),
            pltpu.VMEM((p.gx, p.jb, LANES), f32),
            pltpu.VMEM((p.gx, p.jb, LANES), f32),
            pltpu.VMEM((p.n, LANES), f32),
            dma((p.chunks, p.pack)),
            dma((p.chunks, p.gy)),
            dma((p.chunks, p.gy)),
            dma((4, p.gx)),
        ],
        compiler_params=pltpu.CompilerParams(
            collective_id=0, has_side_effects=True, vmem_limit_bytes=40 * 2**20
        ),
        name="forward",
    )(rho, sz, sy, epsj, epsk)


def total_copies(p, src_ref, slots_ref, sems, axis, base):
    size = p.gx if axis == "gx" else p.gy
    me = lax.axis_index(axis)
    out = []
    for d in range(1, size):
        r = lax.rem(me + d, size)
        out.append(remote(src_ref, slots_ref.at[me], sems.at[base, d], sems.at[base + 1, d], {axis: r}))
    return out


def reduce_kernel(p, x_ref, out_ref, stage_ref, sum_ref, xs_ref, ys_ref, sems):
    ix, iy = lax.axis_index("gx"), lax.axis_index("gy")
    stage_ref[...] = x_ref[...]
    xs_ref[ix] = x_ref[...]
    greet(p)
    a = total_copies(p, stage_ref, xs_ref, sems, "gx", 0)
    for c in a:
        c.start()
    for c in a:
        c.wait_recv()
    total = xs_ref[0]
    for i in range(1, p.gx):
        total = total + xs_ref[i]
    sum_ref[...] = total
    ys_ref[iy] = total
    b = total_copies(p, sum_ref, ys_ref, sems, "gy", 2)
    for c in b:
        c.start()
    for c in b:
        c.wait_recv()
    total = ys_ref[0]
    for i in range(1, p.gy):
        total = total + ys_ref[i]
    out_ref[...] = total
    for c in a + b:
        c.wait_send()


def all_sum(p, x):
    f32 = jnp.float32
    vmem = pl.BlockSpec(memory_space=pltpu.VMEM)
    return pl.pallas_call(
        functools.partial(reduce_kernel, p),
        in_specs=[vmem],
        out_specs=vmem,
        out_shape=jax.ShapeDtypeStruct(x.shape, f32),
        scratch_shapes=[
            pltpu.VMEM(x.shape, f32),
            pltpu.VMEM(x.shape, f32),
            pltpu.VMEM((p.gx,) + x.shape, f32),
            pltpu.VMEM((p.gy,) + x.shape, f32),
            pltpu.SemaphoreType.DMA((4, max(p.gx, p.gy))),
        ],
        compiler_params=pltpu.CompilerParams(collective_id=1, has_side_effects=True, vmem_limit_bytes=8 * 2**20),
        name="all_sum",
    )(x)


def backward_kernel(p, rhs_ref, first_ref, tab_ref, sy_ref, sz_ref, out_ref, energy_ref,
                    w_ref, u_ref, carry_ref, left_ref, right_ref, edge_ref, got_ref, back_ref, ends_ref,
                    part_ref, xs_ref, sum_ref, ys_ref, res_ref,
                    write_sems, out_sems, land_sems, line_sems, sum_sems):
    ix, iy = lax.axis_index("gx"), lax.axis_index("gy")
    greet(p)
    edge_sums(p, rhs_ref, tab_ref, left_ref, right_ref, edge_ref)

    ea = total_copies(p, part_ref, xs_ref, sum_sems, "gx", 0)
    eb = total_copies(p, sum_ref, ys_ref, sum_sems, "gy", 2)

    def between(stage):
        if stage == 0:
            energy = jnp.zeros((8, LANES), jnp.float32)
            for i in range(p.sub):
                prod = first_ref[i] * rhs_ref[i]
                for r in range(p.n // 8):
                    energy = energy + prod[r * 8:(r + 1) * 8]
            part_ref[...] = energy
            xs_ref[ix] = energy
            return
        for c in ea:
            c.start()

    line_exchange(p, tab_ref, edge_ref, got_ref, back_ref, ends_ref, line_sems, between)
    for t in range(p.n // p.tile):
        rows = pl.ds(t * p.tile, p.tile)
        lam = tab_ref[0, rows]
        a, b = carries(p, rows, tab_ref, left_ref, right_ref, ends_ref)
        carry_ref[rows] = a
        for i in range(p.sub - 1, -1, -1):
            b = b * lam
            w_ref[i, rows] = b
            b = b + rhs_ref[i, rows]
    for c in ea:
        c.wait_recv()
    total = xs_ref[0]
    for i in range(1, p.gx):
        total = total + xs_ref[i]
    sum_ref[...] = total
    ys_ref[iy] = total

    order = list(range(p.gy // 2, p.gy)) + list(range(1, p.gy // 2))

    def swap(c, d):
        q = lax.rem(iy + d, p.gy)
        planes = pl.ds(c * p.step, p.step)
        return remote(u_ref.at[planes, pl.ds(q * p.cb, p.cb)], res_ref.at[iy, planes],
                      out_sems.at[c, d], land_sems.at[c, d], {"gy": q})

    def across(c, carry):
        for t in range(p.n // p.tile):
            rows = pl.ds(t * p.tile, p.tile)
            lam, inv = tab_ref[0, rows], tab_ref[1, rows]
            a = carry_ref[rows]
            for i in range(p.step):
                s = c * p.step + i
                a = a * lam + rhs_ref[s, rows]
                w_ref[s, rows] = (a + w_ref[s, rows]) * inv
            carry_ref[rows] = a
        for i in range(0, p.step, p.pair):
            s = c * p.step + i
            x = jnp.concatenate([w_ref[s + e] for e in range(p.pair)], axis=1)
            y = left_mul(sy_ref, x)
            for e in range(p.pair):
                u_ref[s + e] = y[:, e * LANES:(e + 1) * LANES]
        planes = pl.ds(c * p.step, p.step)

        @pl.when(c > 0)
        def _():
            for d in order:
                swap(c - 1, d).start()

        res_ref[iy, planes] = u_ref[planes, pl.ds(iy * p.cb, p.cb)]
        return carry

    lax.fori_loop(0, p.chunks, across, 0)
    for c in eb:
        c.start()
    for d in order:
        swap(p.chunks - 1, d).start()

    block = p.step * p.cb

    def write(c, g):
        rows = pl.ds(g * p.sub + c * p.step, p.step)
        return pltpu.make_async_copy(x_view(rows), out_ref.at[rows], write_sems.at[c, g])

    def x_view(rows):
        return fin_ref.at[rows]

    fin_ref = energy_ref[1]

    def finish(c, carry):
        for d in order:
            swap(c, d).wait_recv()
        planes = pl.ds(c * p.step, p.step)
        place = p.lanes(block)
        parts = [res_ref[q, planes].reshape(block, LANES) for q in range(p.gy)]
        per = LANES // p.kb
        rows = []
        for g in range(p.pack):
            cols = []
            for col in range(p.n // LANES):
                acc = None
                for e in range(per):
                    part = turn(parts[col * per + e], (e - g) * p.kb)
                    acc = part if acc is None else jnp.where(place == e, part, acc)
                cols.append(acc)
            rows.append(jnp.concatenate(cols, axis=1))
        y = right_mul(jnp.concatenate(rows, axis=0), sz_ref)
        for g in range(p.pack):
            at = pl.ds(g * p.sub + c * p.step, p.step)
            fin_ref[at] = y[g * block:(g + 1) * block].reshape(p.step, p.cb, p.n)

        @pl.when(c > 0)
        def _():
            for g in range(p.pack):
                write(c - 1, g).start()

        return carry

    lax.fori_loop(0, p.chunks, finish, 0)
    for c in eb:
        c.wait_recv()
    total = ys_ref[0]
    for i in range(1, p.gy):
        total = total + ys_ref[i]
    energy_ref[0][...] = total
    for g in range(p.pack):
        write(p.chunks - 1, g).start()
    for c in range(p.chunks):
        for g in range(p.pack):
            write(c, g).wait()
    for c in ea + eb:
        c.wait_send()

    def drain(c, carry):
        for d in order:
            swap(c, d).wait_send()
        return carry

    lax.fori_loop(0, p.chunks, drain, 0)


def backward_entry(p, rhs_ref, first_ref, tab_ref, sy_ref, sz_ref, out_ref, energy_ref, fin_ref, *rest):
    backward_kernel(p, rhs_ref, first_ref, tab_ref, sy_ref, sz_ref, out_ref, (energy_ref, fin_ref), *rest)


def backward(p, rhs, first, tab, sy, sz):
    f32 = jnp.float32
    cube = (p.sub, p.n, LANES)
    plane = (p.n, LANES)
    vmem = pl.BlockSpec(memory_space=pltpu.VMEM)
    dma = pltpu.SemaphoreType.DMA
    return pl.pallas_call(
        functools.partial(backward_entry, p),
        in_specs=[vmem] * 5,
        out_specs=[pl.BlockSpec(memory_space=pl.ANY), vmem],
        out_shape=[jax.ShapeDtypeStruct((p.ca, p.cb, p.n), f32), jax.ShapeDtypeStruct((8, LANES), f32)],
        scratch_shapes=[
            pltpu.VMEM((p.ca, p.cb, p.n), f32),
            pltpu.VMEM(cube, f32),
            pltpu.VMEM(cube, f32),
            pltpu.VMEM(plane, f32),
            pltpu.VMEM(plane, f32),
            pltpu.VMEM(plane, f32),
            pltpu.VMEM(plane, f32),
            pltpu.VMEM((p.gx, p.jb, LANES), f32),
            pltpu.VMEM((p.gx, p.jb, LANES), f32),
            pltpu.VMEM(plane, f32),
            pltpu.VMEM((8, LANES), f32),
            pltpu.VMEM((p.gx, 8, LANES), f32),
            pltpu.VMEM((8, LANES), f32),
            pltpu.VMEM((p.gy, 8, LANES), f32),
            pltpu.VMEM((p.gy, p.sub, p.cb, LANES), f32),
            dma((p.chunks, p.pack)),
            dma((p.chunks, p.gy)),
            dma((p.chunks, p.gy)),
            dma((4, p.gx)),
            dma((4, max(p.gx, p.gy))),
        ],
        compiler_params=pltpu.CompilerParams(
            collective_id=2, has_side_effects=True, vmem_limit_bytes=40 * 2**20
        ),
        name="backward",
    )(rhs, first, tab, sy, sz)


def shards(charge_density):
    ca, cb, n = charge_density.shape
    gx, gy = lax.axis_size("gx"), lax.axis_size("gy")
    ix, iy = lax.axis_index("gx"), lax.axis_index("gy")
    kb = n // gy
    pack = LANES // kb
    sub = ca // pack
    width = pack * kb
    h = 1.0 / (n + 1)
    norm = (2.0 * h) ** 2

    num = np.arange(n) + 1
    sine64 = np.sin(np.pi * ((num[:, None] * num[None, :]) % (2 * (n + 1))) / (n + 1))
    sine = jnp.asarray(sine64.astype(np.float32))
    eps64 = 4.0 * np.sin(np.pi * num / (2.0 * (n + 1))) ** 2
    cheb64 = np.cos(np.arange(DEG)[None, :] * np.arccos((2.0 * np.arange(n) - (n - 1)) * h)[:, None])
    cheb = jnp.asarray(cheb64.astype(np.float32))
    chebhat = jnp.asarray((sine64 @ cheb64).astype(np.float32))
    tensors, parity = face_tensors()

    epsj = jnp.asarray(np.repeat(eps64.astype(np.float32)[:, None], LANES, axis=1))
    epsk = np.tile(eps64.astype(np.float32).reshape(gy, 1, kb), (1, 8, pack))
    plan = Plan(ca, cb, n, gx, gy)
    sz = split_table(sine64)
    rhs, first, tab = forward(plan, charge_density, sz, split_table(sine64 * h * h), epsj, jnp.asarray(epsk))

    edge_rows = jnp.stack([sine[0], sine[n - 1]])
    edge_k = lax.dynamic_slice_in_dim(edge_rows, iy * kb, kb, 1)
    hat_k = lax.dynamic_slice_in_dim(chebhat, iy * kb, kb, 0)
    cheb_a = lax.dynamic_slice_in_dim(cheb, ix * ca, ca, 0)
    wall_x = jnp.stack([first[0, :, :kb], first[sub - 1, :, width - kb :]])
    own_x = jnp.stack([ix == 0, ix == gx - 1]).astype(jnp.float32)
    wall_x = wall_x * own_x[:, None, None]
    mom_x = jnp.einsum("fjk,jp->fpk", wall_x, chebhat, precision=BEST)
    mom_x = jnp.einsum("fpk,kq->fpq", mom_x, hat_k, precision=BEST)
    wall_y = jnp.sum(first[None] * edge_rows[:, None, :, None], axis=2)
    wall_y = wall_y.reshape(2, sub, pack, kb).transpose(0, 2, 1, 3).reshape(2, ca, kb)
    mom_y = jnp.einsum("fak,ap->fpk", wall_y, cheb_a, precision=BEST)
    mom_y = jnp.einsum("fpk,kq->fpq", mom_y, hat_k, precision=BEST)
    edge_lane = jnp.einsum("fk,gh->gkfh", edge_k, jnp.eye(pack, dtype=jnp.float32)).reshape(width, 2 * pack)
    wall_z = jnp.einsum("sjl,lc->csj", first, edge_lane, precision=HIGH)
    wall_z = wall_z.reshape(2, ca, n)
    mom_z = jnp.einsum("faj,jq->faq", wall_z, chebhat, precision=BEST)
    mom_z = jnp.einsum("faq,ap->fpq", mom_z, cheb_a, precision=BEST)
    moments = jnp.stack([mom_x, mom_y, mom_z]).reshape(-1) * (h * norm)
    energy_one = h * norm * jnp.sum(first * rhs)
    packed = jnp.concatenate([moments, energy_one[None]])
    fill = -packed.shape[0] % (8 * LANES)
    packed = all_sum(plan, jnp.pad(packed, (0, fill)).reshape(-1, LANES)).reshape(-1)[: packed.shape[0]]
    moments = packed[:-1].reshape(3, 2, 1, 1, DEG * DEG)
    energy_one = packed[-1]

    tens = jnp.asarray(tensors)
    par = jnp.asarray(parity)
    gain = jnp.asarray(expansion_weights() * (RADIUS ** -np.arange(DEG, dtype=np.float64))[:, None].astype(np.float32))
    lm = jnp.sum(tens * moments[:, 1], axis=3) + par * jnp.sum(tens * moments[:, 0], axis=3)
    lm = jnp.sum(lm, axis=0) * gain
    coef_hi = jnp.sum(tens * lm[None, :, :, None], axis=2).reshape(3, DEG, DEG, DEG)
    coef_lo = jnp.sum(tens * (par * lm[None])[..., None], axis=2).reshape(3, DEG, DEG, DEG)

    coord = jnp.asarray(((np.arange(n) - (n - 1) / 2.0) * h).astype(np.float32))
    coord_a = lax.dynamic_slice_in_dim(coord, ix * ca, ca)

    def face(coefs, cheb_u, cheb_v, u, v):
        part = jnp.einsum("flpq,up->fluq", coefs, cheb_u, precision=BEST)
        part = jnp.einsum("fluq,vq->fluv", part, cheb_v, precision=HIGH)
        rinv = lax.rsqrt(0.25 + u[:, None] * u[:, None] + v[None, :] * v[None, :])
        acc = part[:, ORDER]
        for l in range(ORDER - 1, -1, -1):
            acc = acc * rinv + part[:, l]
        return acc

    coef_x = jnp.where(ix == 0, coef_lo[0], coef_hi[0])[None]
    phi_x = face(coef_x, cheb, cheb, coord, coord)[0]
    phi_y = face(jnp.stack([coef_lo[1], coef_hi[1]]), cheb_a, cheb, coord_a, coord)
    phi_z = face(jnp.stack([coef_lo[2], coef_hi[2]]), cheb_a, cheb, coord_a, coord)

    sine_k = lax.dynamic_slice_in_dim(sine, iy * kb, kb, 1)
    hat_x = jnp.einsum("yz,zk->yk", phi_x, sine_k, precision=HIGH)
    hat_x = jnp.einsum("jy,yk->jk", sine, hat_x, precision=HIGH)
    hat_y = jnp.einsum("faz,zk->fak", phi_y, sine_k, precision=HIGH)
    hat_z = jnp.einsum("fay,yj->faj", phi_z, sine, precision=HIGH)
    hat_y = hat_y.reshape(2, pack, sub, kb).transpose(0, 2, 1, 3).reshape(2, sub, 1, width)
    add = hat_y[0] * edge_rows[0][None, :, None] + hat_y[1] * edge_rows[1][None, :, None]
    add = add + jnp.einsum(
        "csj,lc->sjl", hat_z.reshape(2 * pack, sub, n), edge_lane, precision=HIGH
    )
    rhs2 = rhs + add
    blank = jnp.zeros((n, width - kb), jnp.float32)
    rhs2 = rhs2.at[0].add(own_x[0] * jnp.concatenate([hat_x, blank], axis=1))
    rhs2 = rhs2.at[sub - 1].add(own_x[1] * jnp.concatenate([blank, hat_x], axis=1))
    potential, energy_two = backward(plan, rhs2, first, tab, split_table(sine64 * norm), sz)
    energy_two = h * norm * jnp.sum(energy_two)
    return potential, jnp.stack([energy_one, energy_two])


def solution(mesh):
    return jax.shard_map(
        shards,
        mesh=mesh,
        in_specs=(P("gx", "gy", None),),
        out_specs=(P("gx", "gy", None), P()),
        check_vma=False,
    )
```

profile of v0, /device:TPU:1, one launch (start us, length us, event | category | flops | bytes accessed | tf_op | source)
XLA Modules:
  0.0 151.8 jit_solution(12110385259870615657)
XLA Ops:
  0.7 0.8 multiply_add_fusion
  1.5 0.1 add.329
  1.6 0.7 constant_dynamic-slice_fusion
  2.3 0.6 fusion.154
  3.0 0.1 reshape.381
  3.1 1.4 add_rsqrt_fusion.1
  4.4 0.8 add_rsqrt_fusion
  5.2 0.6 mul.538
  5.8 1.6 %copy-done.2 = f32[32,64,256]{2,1,0:T(8,128)S(1)} copy-done((f32[32,64,256]{2,1,0:T(8,128)S(1)}, f32[32,64,256]{2,1,0:T(8,128)}, u32[]{:S(2)}) %copy-start.2) | copy-done | bytes 2097176
  7.4 0.9 copy-done.4
  8.4 0.9 copy-done.6
  9.3 0.9 copy-done.8
  10.2 0.7 copy-done.9
  10.9 43.9 %forward.1 = (f32[16,256,128]{2,1,0:T(8,128)S(1)}, f32[16,256,128]{2,1,0:T(8,128)S(1)}, f32[6,256,128]{2,1,0:T(8,128)S(1)}) custom-call(f32[32,64,256]{2,1,0:T(8,128)S(1)} %copy-done.2, bf16[2,256,256]{2,1,0:T(8,128)(2,1)S(1)} %copy-done.4, bf16[2,256,256]{2,1,0:T(8,128)(2,1)S(1)} %copy-done.6, f32[256,128]{1,0:T(8,128)S(1)} %copy-done.8, ...), custom_call_target="tpu_custom_call" | custom-call | tf_op jit(solution)/shard_map/forward/pallas_call | solution.py:316
  54.9 1.3 copy-done
  56.2 1.2 multiply_reduce_fusion.5
  58.1 0.4 multiply_reduce_fusion
  58.5 0.1 reshape.368
  58.6 0.2 convolution_bitcast_fusion.7
  58.8 0.2 convolution_bitcast_fusion.6
  59.0 0.9 fusion.155
  60.0 0.2 fusion.156
  60.3 0.3 convolution_bitcast_fusion.5
  60.5 0.1 fusion.149
  60.7 0.3 convolution_bitcast_fusion.9
  61.0 0.2 convolution_bitcast_fusion.8
  61.3 0.2 mul.492
  61.5 10.0 %all_sum.1 = f32[16,128]{1,0:T(8,128)S(1)} custom-call(f32[16,128]{1,0:T(8,128)S(1)} %fusion.137.x_ref), custom_call_target="tpu_custom_call" | custom-call | tf_op jit(solution)/shard_map/all_sum/pallas_call | solution.py:388
  71.5 0.6 slice.409
  72.1 0.1 reshape.374
  72.3 2.7 %multiply_reduce_fusion.3 = (f32[3,17,33]{2,1,0:T(8,128)S(1)}, f32[3,17,33]{2,1,0:T(8,128)S(1)}) fusion(f32[3,17,33,289]{3,2,1,0:T(8,128)} %constant.111.clone, f32[3,289]{1,0:T(4,128)S(1)} %get-tuple-element.87, f32[3,289]{1,0:T(4,128)S(1)} %get-tuple-element.88), kind=kLoop, calls=%fused_computation.3 | loop fusion | flops 1942182 | bytes 1965948 | tf_op jit(solution)/shard_map/reduce_sum | solution.py:649
  75.1 1.2 multiply_reduce_fusion.2
  76.3 0.7 slice_select_fusion
  76.9 0.1 select_n.26
  77.0 1.3 convolution_bitcast_fusion.1
  78.3 0.9 slice.301
  79.2 0.9 copy.61
  80.1 1.6 %slice.278 = f32[1,17,17,17]{3,2,0,1:T(8,128)} reshape(f32[1,17,289]{2,1,0:T(8,128)} %get-tuple-element.78) | data formatting | bytes 39304 | tf_op jit(solution)/shard_map/slice | solution.py:668
  81.7 1.1 copy.57
  82.8 1.6 %slice.303 = f32[1,17,17,17]{3,2,0,1:T(8,128)} reshape(f32[1,17,289]{2,1,0:T(8,128)} %get-tuple-element.79) | data formatting | bytes 39304 | tf_op jit(solution)/shard_map/slice | solution.py:669
  84.4 1.8 %copy.62 = f32[1,17,17,17]{2,3,1,0:T(8,128)} copy(f32[1,17,17,17]{3,2,0,1:T(8,128)} %slice.303) | data formatting | bytes 39304 | tf_op jit(solution)/shard_map/slice | solution.py:669
  86.2 2.4 %convolution_bitcast_fusion.2 = f32[2,17,32,17]{2,3,1,0:T(8,128)} fusion(f32[1,17,17,17]{2,3,1,0:T(8,128)} %copy.62, f32[1,17,17,17]{2,3,1,0:T(8,128)} %copy.61, f32[256,17]{0,1:T(8,128)} %constant.106.clone, s32[]{:T(128)S(6)} %select_n.22), kind=kOutput, calls=%fused_computation.9 | convolution fusion | flops 3783010 | bytes 504068 | tf_op jit(solution)/shard_map/flpq,up->fluq/dot_general | solution.py:658
  88.5 0.8 slice.280
  89.3 1.8 %copy.58 = f32[1,17,17,17]{2,3,1,0:T(8,128)} copy(f32[1,17,17,17]{3,2,0,1:T(8,128)} %slice.280) | data formatting | bytes 39304 | tf_op jit(solution)/shard_map/slice | solution.py:668
  91.2 1.5 convolution_bitcast_fusion.3
  92.7 1.4 fusion.157
  94.1 0.1 fusion.151
  94.2 1.1 convolution_bitcast_fusion.4
  95.3 0.1 mul.528
  95.5 1.7 %fusion.158 = f32[2,17,32,256]{3,2,1,0:T(8,128)S(1)} fusion(f32[2,17,32,17]{2,3,1,0:T(8,128)} %convolution_bitcast_fusion.2, f32[256,17,1,1]{0,1,3,2:T(8,128)S(1)} %copy-done.19), kind=kOutput, calls=%fused_computation.197 | convolution fusion | flops 28409856 | bytes 1205504 | tf_op jit(solution)/shard_map/fluq,vq->fluv/dot_general | solution.py:659
  97.3 0.1 fusion.150
  97.4 0.3 fusion.67
  97.7 1.1 copy-done.1
  98.8 2.3 %add_add_fusion = f32[16,256,128]{2,1,0:T(8,128)S(1)} fusion(f32[16,256,128]{2,1,0:T(8,128)S(1)} %copy-done.1, f32[128,4,1]{0,1,2:T(4,128)S(1)} %reshape.381, f32[256]{0:T(256)S(1)} %copy-done.24, f32[16,128]{1,0:T(8,128)S(1)} %mul.533, f32[256]{0:T(256)S(1)} %copy-done.25, f32[16,128]{1,0:T(8,128)S(1)} %mul.528, f32[4,16,256]{2,1,0:T(8,128)S(1)} %fusion.67), kind=kOutput, calls=%fused_computation.6 | convolution fusion | flops 15204352 | bytes 4280320 | tf_op jit(solution)/shard_map/csj,lc->sjl/dot_general | solution.py:678
  101.2 2.1 %convolution_bitcast_fusion = f32[1,17,256,256]{3,2,1,0:T(8,128)S(1)} fusion(f32[17,256,17]{1,2,0:T(8,128)S(1)} %convolution_bitcast_fusion.1, f32[256,17,1]{0,1,2:T(8,128)S(1)} %copy-done.16), kind=kOutput, calls=%fused_computation.5 | convolution fusion | flops 113639424 | bytes 4769792 | tf_op jit(solution)/shard_map/fluq,vq->fluv/dot_general | solution.py:659
  103.4 0.6 fusion.7
  104.0 0.4 fusion.159
  104.4 0.7 fusion.61
  105.0 0.7 fusion.60.rhs_ref
  105.8 39.1 %backward.1 = (f32[32,64,256]{2,1,0:T(8,128)S(1)}, f32[8,128]{1,0:T(8,128)S(1)}) custom-call(f32[16,256,128]{2,1,0:T(8,128)S(1)} %fusion.60.rhs_ref, f32[16,256,128]{2,1,0:T(8,128)S(1)} %get-tuple-element.32.first_ref, f32[6,256,128]{2,1,0:T(8,128)S(1)} %get-tuple-element.33.tab_ref, bf16[2,256,256]{2,1,0:T(8,128)(2,1)S(1)} %copy-done.7, ...), custom_call_target="tpu_custom_call" | custom-call | tf_op jit(solution)/shard_map/backward/pallas_call | solution.py:560
  144.9 1.3 copy-done.3
  146.3 0.6 reduce_sum.79
  147.5 1.1 pad_maximum_fusion
  148.7 3.1 %copy.88 = f32[32,64,256]{2,1,0:T(8,128)} copy(f32[32,64,256]{2,1,0:T(8,128)} %copy-done.3) | data formatting | bytes 4194304
  (62 shorter events, 0.5 us)
Async XLA Ops:
  5.8 1.6 %copy-start.2 = (f32[32,64,256]{2,1,0:T(8,128)S(1)}, f32[32,64,256]{2,1,0:T(8,128)}, u32[]{:S(2)}) copy-start(f32[32,64,256]{2,1,0:T(8,128)} %rho_ref.1) | copy-start | bytes 6291460
  7.4 0.9 copy-start.4
  8.4 0.9 copy-start.6
  9.3 0.9 copy-start.8
  10.2 0.7 copy-start.9
  54.9 1.3 copy-start
  56.2 1.8 %copy-start.22 = (f32[2,256]{1,0:T(2,128)S(1)}, f32[2,256]{1,0:T(2,128)}, u32[]{:S(2)}) copy-start(f32[2,256]{1,0:T(2,128)} %constant.138) | copy-start | bytes 6148
  57.4 1.2 copy-start.18
  57.4 1.4 copy-start.20
  58.1 1.9 %copy-start.17 = (f32[256,17,1]{0,1,2:T(8,128)S(1)}, f32[256,17,1]{0,1,2:T(8,128)}, u32[]{:S(2)}) copy-start(f32[256,17,1]{0,1,2:T(8,128)} %constant.150) | copy-start | bytes 52228
  60.6 14.4 %copy-start.14 = (f32[3,17,33]{2,1,0:T(8,128)S(1)}, f32[3,17,33]{2,1,0:T(8,128)}, u32[]{:S(2)}) copy-start(f32[3,17,33]{2,1,0:T(8,128)} %constant.112.clone) | copy-start | bytes 20200
  60.7 14.4 %copy-start.21 = (f32[17,33]{1,0:T(8,128)S(1)}, f32[17,33]{1,0:T(8,128)}, u32[]{:S(2)}) copy-start(f32[17,33]{1,0:T(8,128)} %constant.113.clone) | copy-start | bytes 6736
  72.2 2.8 %copy-start.10 = (f32[3,17,33,289]{3,2,1,0:T(8,128)S(1)}, f32[3,17,33,289]{3,2,1,0:T(8,128)}, u32[]{:S(2)}) copy-start(f32[3,17,33,289]{3,2,1,0:T(8,128)} %constant.111.clone) | copy-start | bytes 5836648
  92.6 1.6 %copy-start.15 = (f32[2,16,256]{2,1,0:T(8,128)S(1)}, f32[2,16,256]{2,1,0:T(8,128)}, u32[]{:S(2)}) copy-start(f32[2,16,256]{2,1,0:T(8,128)} %add_rsqrt_fusion.1) | copy-start | bytes 98308
  94.1 1.5 copy-start.19
  95.3 2.1 %copy-start.12 = (f32[2,32,256]{2,1,0:T(8,128)S(1)}, f32[2,32,256]{2,1,0:T(8,128)}, u32[]{:S(2)}) copy-start(f32[2,32,256]{2,1,0:T(8,128)} %mul.538) | copy-start | bytes 196612
  95.5 1.9 %copy-start.13 = (f32[256,256,1]{0,1,2:T(8,128)S(1)}, f32[256,256,1]{0,1,2:T(8,128)}, u32[]{:S(2)}) copy-start(f32[256,256,1]{0,1,2:T(8,128)} %constant.152) | copy-start | bytes 786436
  97.2 1.6 %copy-start.1 = (f32[16,256,128]{2,1,0:T(8,128)S(1)}, f32[16,256,128]{2,1,0:T(8,128)}, u32[]{:S(2)}) copy-start(f32[16,256,128]{2,1,0:T(8,128)} %copy-done) | copy-start | bytes 6291460
  97.2 1.6 %copy-start.24 = (f32[256]{0:T(256)S(1)}, f32[256]{0:T(256)}, u32[]{:S(2)}) copy-start(f32[256]{0:T(256)} %constant.141) | copy-start | bytes 3076
  97.3 1.6 %copy-start.25 = (f32[256]{0:T(256)S(1)}, f32[256]{0:T(256)}, u32[]{:S(2)}) copy-start(f32[256]{0:T(256)} %constant.140) | copy-start | bytes 3076
  98.8 2.3 %copy-start.16 = (f32[256,17,1]{0,1,2:T(8,128)S(1)}, f32[256,17,1]{0,1,2:T(8,128)}, u32[]{:S(2)}) copy-start(f32[256,17,1]{0,1,2:T(8,128)} %constant.153) | copy-start | bytes 52228
  101.1 2.2 %copy-start.11 = (f32[256,256]{0,1:T(8,128)S(1)}, f32[256,256]{0,1:T(8,128)}, u32[]{:S(2)}) copy-start(f32[256,256]{0,1:T(8,128)} %constant.105.clone) | copy-start | bytes 786436
  101.1 2.2 %copy-start.23 = (f32[256]{0:T(256)S(1)}, f32[256]{0:T(256)}, u32[]{:S(2)}) copy-start(f32[256]{0:T(256)} %constant.139) | copy-start | bytes 3076
  101.2 2.2 %copy-start.26 = (f32[256]{0:T(256)S(1)}, f32[256]{0:T(256)}, u32[]{:S(2)}) copy-start(f32[256]{0:T(256)} %constant.142) | copy-start | bytes 3076
  103.3 2.4 %copy-start.5 = (bf16[2,256,256]{2,1,0:T(8,128)(2,1)S(1)}, bf16[2,256,256]{2,1,0:T(8,128)(2,1)}, u32[]{:S(2)}) copy-start(bf16[2,256,256]{2,1,0:T(8,128)(2,1)} %constant.128.sz_ref) | copy-start | bytes 786436
  103.4 2.4 %copy-start.7 = (bf16[2,256,256]{2,1,0:T(8,128)(2,1)S(1)}, bf16[2,256,256]{2,1,0:T(8,128)(2,1)}, u32[]{:S(2)}) copy-start(bf16[2,256,256]{2,1,0:T(8,128)(2,1)} %constant.149.sy_ref) | copy-start | bytes 786436
  144.9 1.3 copy-start.3
where the time goes:
time: 153 us; the launch traced here: 152 us
  Pallas kernels  93.1 us (61%)
  local copies, waits for them, and re-layouts  26.3 us (17%)
  matrix products  17.4 us (11%)
  other arithmetic  12.4 us (8%)
  between operations  2.56 us (2%)
    pallas_call x1, Pallas kernels, forward(): pl.pallas_call(functools.partial(forward_kernel, p), in_specs=[pl.BlockSp...  43.9 us
    pallas_call x1, Pallas kernels, backward(): pl.pallas_call(functools.partial(backward_entry, p), in_specs=[vmem] * 5,...  39.1 us
    unnamed x56, local copies, waits for them, and re-layouts  12.1 us
    pallas_call x1, Pallas kernels, all_sum(): pl.pallas_call(functools.partial(reduce_kernel, p), in_specs=[vmem], out_...  10 us
    dot_general x3, matrix products, face(): part = jnp.einsum('fluq,vq->fluv', part, cheb_v, precision=HIGH)  5.25 us
    dot_general x3, matrix products, face(): part = jnp.einsum('flpq,up->fluq', coefs, cheb_u, precision=BEST)  5.11 us
    slice x2, local copies, waits for them, and re-layouts, shards(): coef_hi[2]  3.38 us

commit v1 on v0

v1 whole, which is shorter than its diff:
```python
import functools
import math

import jax
import jax.numpy as jnp
import numpy as np
from jax import lax
from jax.experimental import pallas as pl
from jax.experimental.pallas import tpu as pltpu
from jax.sharding import PartitionSpec as P

ORDER = 16
DEG = ORDER + 1
RATIO = 1.1
RADIUS = math.sqrt(3.0) / 2.0
LANES = 128
MESH = pl.DeviceIdType.MESH
BF16 = jnp.bfloat16
EVEN = -(-((DEG + 1) // 2) // 8) * 8
ROWS = EVEN + -(-(DEG // 2) // 8) * 8
BLOCK = 32
PER = LANES // BLOCK
NBLK = -(-DEG // PER)
MI = (DEG + 1) // 2


def solid_harmonics(x, y, z):
    rr = x * x + y * y + z * z
    out = np.zeros((DEG, 2 * DEG - 1) + x.shape)
    cos = np.zeros((DEG, DEG) + x.shape)
    sin = np.zeros((DEG, DEG) + x.shape)
    cos[0, 0] = 1.0
    for l in range(1, DEG):
        s = 1.0 if l == 1 else math.sqrt((2 * l - 1) / (2.0 * l))
        cos[l, l] = s * (x * cos[l - 1, l - 1] - y * sin[l - 1, l - 1])
        sin[l, l] = s * (x * sin[l - 1, l - 1] + y * cos[l - 1, l - 1])
        for m in range(l):
            div = math.sqrt(l * l - m * m)
            far = math.sqrt((l - 1) * (l - 1) - m * m) if l - 1 > m else 0.0
            for f in (cos, sin):
                f[l, m] = (2 * l - 1) * z * f[l - 1, m] / div
                if l >= 2 and far:
                    f[l, m] = f[l, m] - far * rr * f[l - 2, m] / div
    out[:, :DEG] = cos
    out[:, DEG:] = sin[:, 1:]
    return out


def face_tensors():
    t = np.cos(np.pi * (np.arange(DEG) + 0.5) / DEG)
    fwd = np.cos(np.arange(DEG)[:, None] * np.arccos(t)[None, :]) * (2.0 / DEG)
    fwd[0] *= 0.5
    u, v = np.meshgrid(t / 2, t / 2, indexing="ij")
    half = np.full_like(u, 0.5)
    tensors = []
    for pts in ((half, u, v), (u, half, v), (u, v, half)):
        vals = solid_harmonics(*pts)
        tensors.append(np.einsum("pu,lfuv,qv->lfpq", fwd, vals, fwd))
    return np.stack(tensors)


def expansion_weights():
    w = np.zeros((DEG, 2 * DEG - 1))
    for l in range(DEG):
        for f in range(2 * DEG - 1):
            m = f if f < DEG else f - ORDER
            w[l, f] = (1.0 if m == 0 else 2.0) / (4.0 * math.pi * RADIUS * RATIO ** (l + 1))
    return w.astype(np.float32)


def split(x):
    hi = x.astype(jnp.bfloat16)
    return hi, (x - hi.astype(jnp.float32)).astype(jnp.bfloat16)


def dot(a, b):
    return jnp.dot(a, b, preferred_element_type=jnp.float32)


def left_mul(mat, x):
    hi, lo = split(x)
    return dot(mat[0], hi) + dot(mat[0], lo) + dot(mat[1], hi)


def right_mul(x, mat):
    hi, lo = split(x)
    return dot(hi, mat[0]) + dot(lo, mat[0]) + dot(hi, mat[1])


def dot_t(a, b):
    return lax.dot_general(a, b, (((1,), (1,)), ((), ())), preferred_element_type=jnp.float32)


def split_table(table):
    t = np.asarray(table, np.float32)
    hi = t.astype(BF16)
    return hi, (t - hi.astype(np.float32)).astype(BF16)


def turn(x, shift):
    width = x.shape[-1]
    shift %= width
    return pltpu.roll(x, shift, x.ndim - 1) if shift else x


class Plan:
    def __init__(self, ca, cb, n, gx, gy):
        self.ca, self.cb, self.n, self.gx, self.gy = ca, cb, n, gx, gy
        self.kb = n // gy
        self.h = 1.0 / (n + 1)
        self.norm = (2.0 * self.h) ** 2
        self.jb = n // gx
        self.width = LANES
        self.pack = LANES // self.kb
        self.sub = ca // self.pack
        self.step = max(1, self.sub // 8)
        self.pair = 2 if self.step % 2 == 0 else 1
        self.chunks = self.sub // self.step
        self.tile = min(n, 64)

    def lanes(self, rows):
        return lax.broadcasted_iota(jnp.int32, (rows, LANES), 1) // self.kb


def greet(p):
    ix, iy = lax.axis_index("gx"), lax.axis_index("gy")
    barrier = pltpu.get_barrier_semaphore()
    for d in range(1, p.gx):
        pl.semaphore_signal(barrier, inc=1, device_id={"gx": lax.rem(ix + d, p.gx)}, device_id_type=MESH)
    for d in range(1, p.gy):
        pl.semaphore_signal(barrier, inc=1, device_id={"gy": lax.rem(iy + d, p.gy)}, device_id_type=MESH)
    pl.semaphore_wait(barrier, p.gx + p.gy - 2)


def remote(src, dst, send, recv, where):
    return pltpu.make_async_remote_copy(
        src_ref=src, dst_ref=dst, send_sem=send, recv_sem=recv, device_id=where, device_id_type=MESH
    )


def mode_tables(p, epsj_ref, epsk_ref, tab_ref):
    iy = lax.axis_index("gy")
    sigma = epsj_ref[0] + epsk_ref[iy][0:1]
    s = 0.5 * jnp.sqrt(sigma)
    t = jnp.sqrt(1.0 + s * s)
    theta = 2.0 * jnp.log1p(s + s * s / (1.0 + t))
    lam = jnp.exp(-theta)
    tab_ref[0] = lam
    tab_ref[1] = p.h * p.h / (4.0 * s * t)
    tab_ref[2] = jnp.exp(-theta * float(p.sub))
    tab_ref[3] = jnp.exp(-theta * float(p.ca))
    tab_ref[4] = lam / (1.0 - jnp.exp(-theta * (2.0 * (p.n + 1))))
    tab_ref[5] = jnp.exp(-theta * float(p.n + 1))


def edge_sums(p, v_ref, tab_ref, left_ref, right_ref, edge_ref):
    for t in range(p.n // p.tile):
        rows = pl.ds(t * p.tile, p.tile)
        lam, lsub = tab_ref[0, rows], tab_ref[2, rows]
        left, right = v_ref[0, rows], v_ref[p.sub - 1, rows]
        for i in range(1, p.sub):
            left = left * lam + v_ref[i, rows]
            right = right * lam + v_ref[p.sub - 1 - i, rows]
        left_ref[rows] = left
        right_ref[rows] = right
        dev_l, dev_r = left, right
        for g in range(1, p.pack):
            dev_l = dev_l * lsub + turn(left, -g * p.kb)
            dev_r = dev_r * lsub + turn(right, g * p.kb)
        edge_ref[rows] = jnp.where(p.lanes(p.tile) == 0, dev_l, dev_r)


def line_exchange(p, tab_ref, edge_ref, got_ref, back_ref, ends_ref, sems, between):
    ix = lax.axis_index("gx")
    mine = pl.ds(ix * p.jb, p.jb)

    def copies(src, dst, base):
        out = []
        for d in range(1, p.gx):
            r = lax.rem(ix + d, p.gx)
            out.append(remote(src(r), dst, sems.at[base, d], sems.at[base + 1, d], {"gx": r}))
        return out

    first = copies(lambda r: edge_ref.at[pl.ds(r * p.jb, p.jb)], got_ref.at[ix], 0)
    for c in first:
        c.start()
    got_ref[ix] = edge_ref[mine]
    between(0)
    for c in first:
        c.wait_recv()
    lower = p.lanes(p.jb) == 0
    blk, det, lnp = tab_ref[3, mine], tab_ref[4, mine], tab_ref[5, mine]
    state = jnp.zeros((p.jb, LANES), jnp.float32)
    states = []
    for t in range(p.gx):
        states.append(state)
        state = state * blk + jnp.where(lower, got_ref[t], got_ref[p.gx - 1 - t])
    other = jnp.where(lower, turn(state, p.kb), turn(state, -p.kb))
    image = (other - state * lnp) * det
    for t in range(p.gx):
        states[t] = states[t] - image
        image = image * blk
    for t in range(p.gx):
        back_ref[t] = jnp.where(lower, states[t], states[p.gx - 1 - t])
    second = copies(lambda r: back_ref.at[r], ends_ref.at[mine], 2)
    for c in second:
        c.start()
    ends_ref[mine] = back_ref[ix]
    between(1)
    for c in second:
        c.wait_recv()
    for c in first + second:
        c.wait_send()


def carries(p, rows, tab_ref, left_ref, right_ref, ends_ref):
    lsub = tab_ref[2, rows]
    left, right = left_ref[rows], right_ref[rows]
    a = b = ends_ref[rows]
    place = p.lanes(p.tile)
    for g in range(p.pack - 1):
        a = jnp.where(place == g + 1, turn(a * lsub + left, p.kb), a)
        h = p.pack - 1 - g
        b = jnp.where(place == h - 1, turn(b * lsub + right, -p.kb), b)
    return a, b


def row_degrees():
    deg = np.full(ROWS, -1)
    deg[: (DEG + 1) // 2] = np.arange(0, DEG, 2)
    deg[EVEN : EVEN + DEG // 2] = np.arange(1, DEG, 2)
    return deg


def harmonic_tables(p):
    tens = face_tensors()
    deg = row_degrees()
    weights = expansion_weights() * (RADIUS ** -np.arange(DEG, dtype=np.float64))[:, None] * (p.norm / p.h)
    big = np.zeros((3, MI, ROWS, NBLK * LANES))
    sign = np.ones((3, ROWS, NBLK * LANES))
    gain = np.zeros((2, NBLK, 16, LANES))
    for l in range(DEG):
        for face in range(3):
            for i in range(ROWS):
                r = deg[i]
                if r < 0:
                    continue
                for q in range(DEG):
                    if face == 0:
                        odd, mpar = r % 2, (l - q) % 2
                    elif face == 1:
                        mpar = (l - q) % 2
                        odd = (r + mpar) % 2
                    else:
                        odd = q % 2
                        mpar = (r + odd) % 2
                    at = l * BLOCK + q
                    sign[face, i, at] = (-1.0) ** (mpar + odd, odd, l + mpar)[face]
                    for mi in range(MI):
                        m = mpar + 2 * mi
                        if m <= l and not (odd and m == 0):
                            big[face, mi, i, at] = tens[face, l, ORDER + m if odd else m][r, q]
        for c in range(2):
            for odd in range(2):
                for mi in range(MI):
                    m = (l - c) % 2 + 2 * mi
                    if m <= l:
                        at = (l % PER) * BLOCK + c
                        gain[odd, l // PER, mi, at : (l % PER + 1) * BLOCK : 2] = weights[l, m]
    return big.astype(np.float32), sign.astype(np.float32), gain.astype(np.float32)


def tables(p):
    n = p.n
    num = np.arange(n) + 1
    sine = np.sin(np.pi * ((num[:, None] * num[None, :]) % (2 * (n + 1))) / (n + 1))
    eps = 4.0 * np.sin(np.pi * num / (2.0 * (n + 1))) ** 2
    cheb = np.cos(np.arange(DEG)[None, :] * np.arccos((2.0 * np.arange(n) - (n - 1)) * p.h)[:, None])
    hat = sine @ cheb
    deg = row_degrees()
    used = deg >= 0
    jtab = np.stack([np.repeat(v[:, None], LANES, axis=1) for v in (eps, sine[0])])
    ktab = np.zeros((p.gy, 8, LANES))
    for r, v in enumerate((eps, sine[0], sine[n - 1])):
        ktab[:, r] = np.tile(v.reshape(p.gy, p.kb), (1, p.pack))
    wide = np.zeros((ROWS + 8, n))
    wide[:ROWS][used] = hat[:, deg[used]].T
    wide[ROWS], wide[ROWS + 1] = sine[0], sine[n - 1]
    lanes = np.zeros((n, LANES))
    for i in range(PER):
        lanes[:, i * BLOCK : i * BLOCK + DEG] = hat
    rows = np.zeros((n, BLOCK))
    rows[:, :ROWS][:, used] = cheb[:, deg[used]]
    rh, rl = split_table(rows)
    cols = np.zeros((BLOCK, n))
    cols[:DEG] = cheb.T
    ch, cl = split_table(cols)
    same = np.arange(LANES)
    same = (same[:, None] // BLOCK == same[None, :] // BLOCK) & ((same[:, None] - same[None, :]) % 2 == 0)
    big, sign, gain = harmonic_tables(p)
    f32 = np.float32
    return [
        np.stack(split_table(sine)),
        jtab.astype(f32),
        ktab.astype(f32),
        np.stack(split_table(wide)),
        lanes.astype(f32),
        np.concatenate([rh, rl, rh, np.zeros_like(rh)], axis=1),
        np.concatenate([ch, ch, cl, np.zeros_like(ch)], axis=0),
        big,
        sign,
        gain,
        same.astype(BF16),
    ]


def iota(shape, dim):
    return lax.broadcasted_iota(jnp.int32, shape, dim)


def face_prep(p, dmat_ref, rx_ref, ra_ref):
    ix = lax.axis_index("gx")
    shape = (p.sub, LANES)
    cell = ix * p.ca + (iota(shape, 1) // p.kb) * p.sub + iota(shape, 0)
    t = (2 * cell - (p.n - 1)).astype(jnp.float32) * p.h
    prev, cur = jnp.ones(shape, jnp.float32), t
    dmat_ref[0] = prev
    for d in range(1, DEG):
        dmat_ref[d] = cur
        prev, cur = cur, 2.0 * t * cur - prev
    def inverse_radius(rows, start):
        u = (2 * (start + iota((rows, p.n), 0)) - (p.n - 1)).astype(jnp.float32) * (0.5 * p.h)
        v = (2 * iota((rows, p.n), 1) - (p.n - 1)).astype(jnp.float32) * (0.5 * p.h)
        return lax.rsqrt(0.25 + u * u + v * v)
    rx_ref[...] = inverse_radius(p.n, 0)
    ra_ref[...] = inverse_radius(p.ca, ix * p.ca)


def moments(p, first_ref, rhs_ref, w_ref, v_ref, ktab_ref, dmat_ref, g_ref, y_ref, pay_ref):
    ix, iy = lax.axis_index("gx"), lax.axis_index("gy")
    pair = 2 if p.sub % 2 == 0 else 1
    energy = jnp.zeros((8, LANES), jnp.float32)
    for s in range(0, p.sub, pair):
        x = jnp.concatenate([first_ref[s + e] for e in range(pair)], axis=1)
        y = left_mul(w_ref, x)
        for e in range(pair):
            g_ref[s + e] = y[:, e * LANES:(e + 1) * LANES]
    for s in range(p.sub):
        prod = first_ref[s] * rhs_ref[s]
        for r in range(p.n // 8):
            energy = energy + prod[r * 8:(r + 1) * 8]
    y_ref[...] = jnp.zeros_like(y_ref)
    row_of = {d: i for i, d in enumerate(row_degrees()) if d >= 0}
    lane = iota((ROWS, LANES), 1)
    edge = [ktab_ref[iy][1:2], ktab_ref[iy][2:3]]
    mz = jnp.zeros((ROWS, LANES), jnp.float32)
    for d in range(DEG):
        acc = g_ref[0] * dmat_ref[d, 0:1]
        for s in range(1, p.sub):
            acc = acc + g_ref[s] * dmat_ref[d, s:s + 1]
        for f in range(2):
            at = f * ROWS + row_of[d]
            y_ref[at:at + 1] = acc[ROWS + f:ROWS + f + 1]
            total = jnp.sum(acc[:ROWS] * edge[f], axis=1, keepdims=True)
            mz = jnp.where(lane == f * BLOCK + d, total, mz)
    place = lane // p.kb
    lo = jnp.where((place == 0) & (ix == 0), g_ref[0][:ROWS], 0.0)
    hi = jnp.where((place == p.pack - 1) & (ix == p.gx - 1), g_ref[p.sub - 1][:ROWS], 0.0)
    x = jnp.concatenate([lo, hi, y_ref[...]], axis=0)
    table = v_ref[pl.ds(pl.multiple_of(iy * p.kb, 16), p.kb)]
    y = right_mul(x, split(jnp.concatenate([table] * p.pack, axis=0)))
    which = lane // BLOCK
    packed = y[0:ROWS]
    for i in range(1, 4):
        packed = jnp.where(which == i, y[i * ROWS:(i + 1) * ROWS], packed)
    pay_ref[0:ROWS] = packed
    pay_ref[ROWS:2 * ROWS] = mz
    pay_ref[2 * ROWS:2 * ROWS + 8] = energy


def sum_slots(ref, count):
    total = ref[0]
    for i in range(1, count):
        total = total + ref[i]
    return total


def total_copies(p, src_ref, slots_ref, sems, axis, base):
    size = p.gx if axis == "gx" else p.gy
    me = lax.axis_index(axis)
    out = []
    for d in range(1, size):
        r = lax.rem(me + d, size)
        out.append(remote(src_ref, slots_ref.at[me], sems.at[base, d], sems.at[base + 1, d], {axis: r}))
    return out


def all_sum(p, pay_ref, xs_ref, sum_ref, ys_ref, sems):
    ix, iy = lax.axis_index("gx"), lax.axis_index("gy")
    a = total_copies(p, pay_ref, xs_ref, sems, "gx", 0)
    for c in a:
        c.start()
    xs_ref[ix] = pay_ref[...]
    for c in a:
        c.wait_recv()
    total = sum_slots(xs_ref, p.gx)
    sum_ref[...] = total
    b = total_copies(p, sum_ref, ys_ref, sems, "gy", 2)
    for c in b:
        c.start()
    ys_ref[iy] = total
    for c in b:
        c.wait_recv()
    for c in a + b:
        c.wait_send()
    return sum_slots(ys_ref, p.gy)


def trade(x):
    odd = iota(x.shape, 1) % 2 == 1
    return jnp.where(odd, turn(x, 1), turn(x, -1))


def coefficients(p, packed, mz, big_ref, sign_ref, gain_ref, same_ref, s_ref, coef_ref):
    which = iota((ROWS, LANES), 1) // BLOCK

    def spread(x, i):
        x = turn(jnp.where(which == i, x, 0.0), -i * BLOCK)
        x = x + turn(x, BLOCK)
        return x + turn(x, 2 * BLOCK)

    tall = (BLOCK, LANES)
    row, col = iota(tall, 0), iota(tall, 1)
    degree = jnp.where(row < EVEN, 2 * row, 2 * (row - EVEN) + 1)
    place = (col % BLOCK == degree).astype(jnp.float32).astype(BF16)
    mz = split(jnp.concatenate([mz, jnp.zeros((BLOCK - ROWS, LANES), jnp.float32)], axis=0))

    def flip(f):
        pick = (col == f * BLOCK + degree).astype(jnp.float32).astype(BF16)
        hi, lo = split(dot_t(pick, mz[0]) + dot_t(pick, mz[1]))
        return (dot(hi, place) + dot(lo, place))[:ROWS]

    pairs = [(spread(packed, 0), spread(packed, 1)), (spread(packed, 2), spread(packed, 3)), (flip(0), flip(1))]
    s_ref[...] = jnp.zeros_like(s_ref)
    for face in range(3):
        lo, hi = pairs[face]
        for blk in range(NBLK):
            cols = slice(blk * LANES, (blk + 1) * LANES)
            both = hi + sign_ref[face][:, cols] * lo
            for mi in range(MI):
                prod = big_ref[face, mi][:, cols] * both
                s_ref[face, 0, blk, mi:mi + 1] = jnp.sum(prod[:EVEN], axis=0, keepdims=True)
                s_ref[face, 1, blk, mi:mi + 1] = jnp.sum(prod[EVEN:], axis=0, keepdims=True)
    hi, lo = split(s_ref[...].reshape(6 * NBLK * 16, LANES))
    spread_sum = (dot(hi, same_ref[...]) + dot(lo, same_ref[...])).reshape(3, 2, NBLK, 16, LANES)
    lane = iota((16, LANES), 1)
    for blk in range(NBLK):
        l = blk * PER + lane // BLOCK
        right = lane % 2 == 1
        cross = (l - lane) % 2 == 1
        sx, sy, sz = spread_sum[0], spread_sum[1], spread_sum[2]
        lm = []
        for b in range(2):
            wide = [jnp.where((lane + b) % 2 == 0, sz[a, blk], trade(sz[a, blk])) for a in range(2)]
            other = jnp.where((l + lane + b) % 2 == 1, wide[1], wide[0])
            lm.append((sx[b, blk] + jnp.where(cross, sy[1 - b, blk], sy[b, blk]) + other) * gain_ref[b, blk])
        rows = [lm, [jnp.where(cross, lm[1 - b], lm[b]) for b in range(2)],
                [jnp.where(right, *[jnp.where((l + a) % 2 == 1, trade(lm[b]), lm[b]) for b in (1, 0)]) for a in range(2)]]
        cols = slice(blk * LANES, (blk + 1) * LANES)
        for face in range(3):
            even = jnp.zeros((EVEN, LANES), jnp.float32)
            odd = jnp.zeros((ROWS - EVEN, LANES), jnp.float32)
            for mi in range(MI):
                t = big_ref[face, mi][:, cols]
                even = even + t[:EVEN] * rows[face][0][mi:mi + 1]
                odd = odd + t[EVEN:] * rows[face][1][mi:mi + 1]
            coef_ref[face, blk] = jnp.concatenate([even, odd], axis=0)


def face_coefs(p, coef_ref, sign_ref, c3_ref):
    ix = lax.axis_index("gx")
    which = iota((ROWS, LANES), 1) // BLOCK
    gap = jnp.zeros((BLOCK - ROWS, LANES), jnp.float32)
    rest = jnp.zeros((LANES - 3 * BLOCK, LANES), jnp.float32)
    for l in range(DEG):
        blk, i = divmod(l, PER)
        cols = slice(blk * LANES, (blk + 1) * LANES)
        for face in range(3):
            hi = coef_ref[face, blk]
            lo = hi * sign_ref[face][:, cols]
            for k, c in enumerate([jnp.where(ix == 0, lo, hi)] if face == 0 else [lo, hi]):
                c = turn(jnp.where(which == i, c, 0.0), -i * BLOCK)
                c = c + turn(c, BLOCK) + turn(c, 2 * BLOCK)
                top = c.astype(BF16).astype(jnp.float32)
                full = jnp.concatenate([top, gap, top, gap, c - top, gap, rest], axis=0)
                c3_ref[l, max(0, 2 * face - 1) + k] = full.astype(BF16)


def triple(e):
    top = e.astype(BF16).astype(jnp.float32)
    return jnp.where(iota(e.shape, 1) // BLOCK == 1, e - top, top).astype(BF16)


def faces(p, c3_ref, cu_ref, vt_ref, rx_ref, ra_ref, fx_ref, fa_ref):
    ix = lax.axis_index("gx")
    edge = (ix == 0) | (ix == p.gx - 1)
    fa_ref[...] = jnp.zeros_like(fa_ref)
    near = pl.ds(pl.multiple_of(ix * p.ca, 16), p.ca)

    @pl.when(edge)
    def _():
        fx_ref[...] = jnp.zeros_like(fx_ref)

        def step(i, carry):
            e = dot(cu_ref[...], c3_ref[DEG - 1 - i, 0])
            fx_ref[...] = fx_ref[...] * rx_ref[...] + dot(triple(e), vt_ref[...])
            return carry

        lax.fori_loop(0, DEG, step, 0)

    def step(i, carry):
        e = dot(cu_ref[near], jnp.concatenate([c3_ref[DEG - 1 - i, k] for k in range(1, 5)], axis=1))
        e = jnp.concatenate([e[:, k * LANES:(k + 1) * LANES] for k in range(4)], axis=0)
        ra = jnp.concatenate([ra_ref[...]] * 4, axis=0)
        fa_ref[...] = fa_ref[...] * ra + dot(triple(e), vt_ref[...])
        return carry

    lax.fori_loop(0, DEG, step, 0)


def add_faces(p, rhs_ref, sine_ref, jtab_ref, ktab_ref, fx_ref, fa_ref):
    ix, iy = lax.axis_index("gx"), lax.axis_index("gy")
    ca = p.ca
    chunk = pl.ds(pl.multiple_of(iy * p.kb, 16), p.kb)
    near = [jnp.concatenate([sine_ref[i, chunk]] * p.pack, axis=0) for i in range(2)]

    def to_lanes(x):
        hi, lo = split(x)
        return dot_t(hi, near[0]) + dot_t(lo, near[0]) + dot_t(hi, near[1])

    @pl.when((ix == 0) | (ix == p.gx - 1))
    def _():
        hat = left_mul(sine_ref, to_lanes(fx_ref[...]))
        place = p.lanes(p.n)
        rhs_ref[0] += jnp.where((place == 0) & (ix == 0), hat, 0.0)
        rhs_ref[p.sub - 1] += jnp.where((place == p.pack - 1) & (ix == p.gx - 1), hat, 0.0)

    hy = to_lanes(fa_ref[0:2 * ca])
    place = p.lanes(p.sub)
    planes = []
    for f in range(2):
        acc = hy[f * ca:f * ca + p.sub]
        for g in range(1, p.pack):
            acc = jnp.where(place == g, hy[f * ca + g * p.sub:f * ca + (g + 1) * p.sub], acc)
        planes.append(acc)
    plus, minus = planes[0] + planes[1], planes[0] - planes[1]

    hi, lo = split(jnp.concatenate([fa_ref[2 * ca:4 * ca]] * (LANES // (2 * ca)), axis=0))
    hz = dot_t(sine_ref[0], hi) + dot_t(sine_ref[1], hi) + dot_t(sine_ref[0], lo)
    top = hz.astype(BF16).astype(jnp.float32)
    both = jnp.where(iota(hz.shape, 1) // (2 * ca) == 1, hz - top, top).astype(BF16)
    top = top.astype(BF16)
    square = (LANES, LANES)
    row, col = iota(square, 0), iota(square, 1)
    edge = jnp.where(row % (2 * ca) < ca, ktab_ref[iy][1:2], ktab_ref[iy][2:3])
    head = edge.astype(BF16).astype(jnp.float32)
    fits = (row % ca) // p.sub == col // p.kb
    first = jnp.where(fits & (row // (2 * ca) < 2), head, 0.0)
    second = jnp.where(fits & (row < 2 * ca), edge - head, 0.0)
    pair = 2 if p.sub % 2 == 0 else 1
    even = iota((p.n, LANES), 0) % 2 == 0
    for s in range(0, p.sub, pair):
        pick = [row % p.sub == s + e for e in range(pair)]
        one = jnp.concatenate([jnp.where(k, first, 0.0).astype(BF16) for k in pick], axis=1)
        two = jnp.concatenate([jnp.where(k, second, 0.0).astype(BF16) for k in pick], axis=1)
        add = dot(both, one) + dot(top, two)
        for e in range(pair):
            at = s + e
            wave = jnp.where(even, plus[at:at + 1], minus[at:at + 1])
            rhs_ref[at] += add[:, e * LANES:(e + 1) * LANES] + jtab_ref[1] * wave


def kernel(p, rho_ref, *refs):
    names = ("sine", "jtab", "ktab", "wide", "lanes", "cu", "vt", "big", "sign", "gain", "same")
    hbm = refs[:len(names)]
    out_ref, energy_ref = refs[len(names):len(names) + 2]
    rest = refs[len(names) + 2:]
    local = rest[:len(names)]
    (x_ref, send_ref, spec_ref, rhs_ref, first_ref, tab_ref, left_ref, right_ref, edge_ref, carry_ref,
     got_ref, back_ref, ends_ref, got2_ref, back2_ref, ends2_ref,
     dmat_ref, rx_ref, ra_ref, g_ref, y_ref, pay_ref, pxs_ref, psum_ref, pys_ref,
     s_ref, coef_ref, c3_ref, fx_ref, fa_ref,
     part_ref, xs_ref, sum_ref, ys_ref, u_ref, res_ref, fin_ref,
     table_sems, in_sems, out_sems, land_sems, back_out_sems, back_land_sems,
     line_sems, line2_sems, pay_sems, sum_sems, write_sems) = rest[len(names):]
    sine_ref, jtab_ref, ktab_ref, wide_ref, lanes_ref, cu_ref, vt_ref, big_ref, sign_ref, gain_ref, same_ref = local
    w_ref = spec_ref
    ix, iy = lax.axis_index("gx"), lax.axis_index("gy")
    order = list(range(p.gy // 2, p.gy)) + list(range(1, p.gy // 2))
    block = p.step * p.cb
    staged = [pltpu.make_async_copy(hbm[i], local[i], table_sems.at[i]) for i in range(len(names))]

    def load(c, g):
        rows = pl.ds(g * p.sub + c * p.step, p.step)
        return pltpu.make_async_copy(rho_ref.at[rows], x_ref.at[rows], in_sems.at[c, g])

    staged[0].start()
    for c in range(p.chunks):
        for g in range(p.pack):
            load(c, g).start()
    for copy in staged[1:]:
        copy.start()
    greet(p)
    staged[0].wait()

    def swap(c, d):
        q = lax.rem(iy + d, p.gy)
        planes = pl.ds(c * p.step, p.step)
        return remote(send_ref.at[q, planes], spec_ref.at[planes, pl.ds(iy * p.cb, p.cb)],
                      out_sems.at[c, d], land_sems.at[c, d], {"gy": q})

    def transform(c, carry):
        for g in range(p.pack):
            load(c, g).wait()
        x = jnp.concatenate(
            [x_ref[pl.ds(g * p.sub + c * p.step, p.step)].reshape(block, p.n) for g in range(p.pack)], axis=0
        )
        y = right_mul(x, sine_ref)
        place = p.lanes(block)
        planes = pl.ds(c * p.step, p.step)
        for q in range(p.gy):
            col, off = divmod(q * p.kb, LANES)
            piece = None
            for g in range(p.pack):
                part = turn(y[g * block:(g + 1) * block, col * LANES:(col + 1) * LANES], g * p.kb - off)
                piece = part if piece is None else jnp.where(place == g, part, piece)
            send_ref[q, planes] = piece.reshape(p.step, p.cb, LANES)

        @pl.when(c > 0)
        def _():
            for d in order:
                swap(c - 1, d).start()

        spec_ref[planes, pl.ds(iy * p.cb, p.cb)] = send_ref[iy, planes]
        return carry

    lax.fori_loop(0, p.chunks, transform, 0)
    staged[1].wait()
    staged[2].wait()
    mode_tables(p, jtab_ref, ktab_ref, tab_ref)
    for d in order:
        swap(p.chunks - 1, d).start()
    face_prep(p, dmat_ref, rx_ref, ra_ref)

    def across(c, carry):
        for d in order:
            swap(c, d).wait_recv()
        for i in range(0, p.step, p.pair):
            s = c * p.step + i
            x = jnp.concatenate([spec_ref[s + e] for e in range(p.pair)], axis=1)
            y = left_mul(sine_ref, x)
            for e in range(p.pair):
                rhs_ref[s + e] = y[:, e * LANES:(e + 1) * LANES]
        return carry

    lax.fori_loop(0, p.chunks, across, 0)
    edge_sums(p, rhs_ref, tab_ref, left_ref, right_ref, edge_ref)
    line_exchange(p, tab_ref, edge_ref, got_ref, back_ref, ends_ref, line_sems, lambda stage: None)

    for t in range(p.n // p.tile):
        rows = pl.ds(t * p.tile, p.tile)
        lam, inv = tab_ref[0, rows], tab_ref[1, rows]
        a, b = carries(p, rows, tab_ref, left_ref, right_ref, ends_ref)
        for i in range(p.sub - 1, -1, -1):
            b = b * lam
            first_ref[i, rows] = b
            b = b + rhs_ref[i, rows]
        for i in range(p.sub):
            a = a * lam + rhs_ref[i, rows]
            first_ref[i, rows] = (a + first_ref[i, rows]) * inv

    def drain(c, carry):
        for d in order:
            swap(c, d).wait_send()
        return carry

    lax.fori_loop(0, p.chunks, drain, 0)
    for copy in staged[3:]:
        copy.wait()

    moments(p, first_ref, rhs_ref, wide_ref, lanes_ref, ktab_ref, dmat_ref, g_ref, y_ref, pay_ref)
    total = all_sum(p, pay_ref, pxs_ref, psum_ref, pys_ref, pay_sems)
    energy_one = jnp.sum(total[2 * ROWS:2 * ROWS + 8])
    coefficients(p, total[:ROWS], total[ROWS:2 * ROWS], big_ref, sign_ref, gain_ref, same_ref, s_ref, coef_ref)
    face_coefs(p, coef_ref, sign_ref, c3_ref)
    faces(p, c3_ref, cu_ref, vt_ref, rx_ref, ra_ref, fx_ref, fa_ref)
    add_faces(p, rhs_ref, sine_ref, jtab_ref, ktab_ref, fx_ref, fa_ref)

    edge_sums(p, rhs_ref, tab_ref, left_ref, right_ref, edge_ref)
    ea = total_copies(p, part_ref, xs_ref, sum_sems, "gx", 0)
    eb = total_copies(p, sum_ref, ys_ref, sum_sems, "gy", 2)

    def between(stage):
        if stage == 0:
            energy = jnp.zeros((8, LANES), jnp.float32)
            for i in range(p.sub):
                prod = first_ref[i] * rhs_ref[i]
                for r in range(p.n // 8):
                    energy = energy + prod[r * 8:(r + 1) * 8]
            part_ref[...] = energy
            xs_ref[ix] = energy
            return
        for c in ea:
            c.start()

    line_exchange(p, tab_ref, edge_ref, got2_ref, back2_ref, ends2_ref, line2_sems, between)
    for t in range(p.n // p.tile):
        rows = pl.ds(t * p.tile, p.tile)
        lam = tab_ref[0, rows]
        a, b = carries(p, rows, tab_ref, left_ref, right_ref, ends2_ref)
        carry_ref[rows] = a
        for i in range(p.sub - 1, -1, -1):
            b = b * lam
            first_ref[i, rows] = b
            b = b + rhs_ref[i, rows]
    for c in ea:
        c.wait_recv()
    total = sum_slots(xs_ref, p.gx)
    sum_ref[...] = total
    ys_ref[iy] = total

    def swap_back(c, d):
        q = lax.rem(iy + d, p.gy)
        planes = pl.ds(c * p.step, p.step)
        return remote(u_ref.at[planes, pl.ds(q * p.cb, p.cb)], res_ref.at[iy, planes],
                      back_out_sems.at[c, d], back_land_sems.at[c, d], {"gy": q})

    def back_across(c, carry):
        for t in range(p.n // p.tile):
            rows = pl.ds(t * p.tile, p.tile)
            lam, inv = tab_ref[0, rows], tab_ref[1, rows] * p.norm
            a = carry_ref[rows]
            for i in range(p.step):
                s = c * p.step + i
                a = a * lam + rhs_ref[s, rows]
                first_ref[s, rows] = (a + first_ref[s, rows]) * inv
            carry_ref[rows] = a
        for i in range(0, p.step, p.pair):
            s = c * p.step + i
            x = jnp.concatenate([first_ref[s + e] for e in range(p.pair)], axis=1)
            y = left_mul(sine_ref, x)
            for e in range(p.pair):
                u_ref[s + e] = y[:, e * LANES:(e + 1) * LANES]
        planes = pl.ds(c * p.step, p.step)

        @pl.when(c > 0)
        def _():
            for d in order:
                swap_back(c - 1, d).start()

        res_ref[iy, planes] = u_ref[planes, pl.ds(iy * p.cb, p.cb)]
        return carry

    lax.fori_loop(0, p.chunks, back_across, 0)
    for c in eb:
        c.start()
    for d in order:
        swap_back(p.chunks - 1, d).start()

    def write(c, g):
        rows = pl.ds(g * p.sub + c * p.step, p.step)
        return pltpu.make_async_copy(fin_ref.at[rows], out_ref.at[rows], write_sems.at[c, g])

    def finish(c, carry):
        for d in order:
            swap_back(c, d).wait_recv()
        planes = pl.ds(c * p.step, p.step)
        place = p.lanes(block)
        parts = [res_ref[q, planes].reshape(block, LANES) for q in range(p.gy)]
        per = LANES // p.kb
        rows = []
        for g in range(p.pack):
            cols = []
            for col in range(p.n // LANES):
                acc = None
                for e in range(per):
                    part = turn(parts[col * per + e], (e - g) * p.kb)
                    acc = part if acc is None else jnp.where(place == e, part, acc)
                cols.append(acc)
            rows.append(jnp.concatenate(cols, axis=1))
        y = right_mul(jnp.concatenate(rows, axis=0), sine_ref)
        for g in range(p.pack):
            at = pl.ds(g * p.sub + c * p.step, p.step)
            fin_ref[at] = y[g * block:(g + 1) * block].reshape(p.step, p.cb, p.n)

        @pl.when(c > 0)
        def _():
            for g in range(p.pack):
                write(c - 1, g).start()

        return carry

    lax.fori_loop(0, p.chunks, finish, 0)
    for c in eb:
        c.wait_recv()
    energy_two = jnp.sum(sum_slots(ys_ref, p.gy))
    for g in range(p.pack):
        write(p.chunks - 1, g).start()
    scale = p.h**3 * p.norm
    energy_ref[...] = jnp.where(iota((8, LANES), 1) == 0, energy_one, energy_two) * scale
    for c in range(p.chunks):
        for g in range(p.pack):
            write(c, g).wait()
    for c in ea + eb:
        c.wait_send()

    def back_drain(c, carry):
        for d in order:
            swap_back(c, d).wait_send()
        return carry

    lax.fori_loop(0, p.chunks, back_drain, 0)


def shards(charge_density):
    ca, cb, n = charge_density.shape
    p = Plan(ca, cb, n, lax.axis_size("gx"), lax.axis_size("gy"))
    f32 = jnp.float32
    data = tables(p)
    cube = (p.sub, p.n, LANES)
    plane = (p.n, LANES)
    slots = (p.gx, p.jb, LANES)
    pay = (2 * ROWS + 8, LANES)
    box = (p.gy, p.sub, p.cb, LANES)
    vmem = lambda shape, dtype=f32: pltpu.VMEM(shape, dtype)
    dma = pltpu.SemaphoreType.DMA
    anywhere = pl.BlockSpec(memory_space=pl.ANY)
    whole = (p.ca, p.cb, p.n)
    scratch = [vmem(t.shape, t.dtype) for t in data]
    scratch += [vmem(whole), vmem(box), vmem(cube), vmem(cube), vmem(cube), vmem((6,) + plane)]
    scratch += [vmem(plane)] * 4
    scratch += [vmem(slots), vmem(slots), vmem(plane)] * 2
    scratch += [vmem((DEG, p.sub, LANES)), vmem((p.n, p.n)), vmem((p.ca, p.n)), vmem((p.sub, ROWS + 8, LANES)),
                vmem((2 * ROWS, LANES)), vmem(pay), vmem((p.gx,) + pay), vmem(pay), vmem((p.gy,) + pay)]
    scratch += [vmem((3, 2, NBLK, 16, LANES)), vmem((3, NBLK, ROWS, LANES)), vmem((DEG, 5, LANES, LANES), BF16),
                vmem((p.n, p.n)), vmem((4 * p.ca, p.n))]
    scratch += [vmem((8, LANES)), vmem((p.gx, 8, LANES)), vmem((8, LANES)), vmem((p.gy, 8, LANES)),
                vmem(cube), vmem(box), vmem(whole)]
    most = max(p.gx, p.gy)
    scratch += [dma((len(data),)), dma((p.chunks, p.pack))] + [dma((p.chunks, p.gy))] * 4
    scratch += [dma((4, p.gx))] * 2 + [dma((4, most))] * 2 + [dma((p.chunks, p.pack))]
    potential, energies = pl.pallas_call(
        functools.partial(kernel, p),
        in_specs=[anywhere] * (1 + len(data)),
        out_specs=[anywhere, pl.BlockSpec(memory_space=pltpu.VMEM)],
        out_shape=[jax.ShapeDtypeStruct(whole, f32), jax.ShapeDtypeStruct((8, LANES), f32)],
        scratch_shapes=scratch,
        compiler_params=pltpu.CompilerParams(
            collective_id=0, has_side_effects=True, vmem_limit_bytes=56 * 2**20
        ),
        name="james",
    )(charge_density, *[jnp.asarray(t) for t in data])
    return potential, energies[0, :2]


def solution(mesh):
    return jax.shard_map(
        shards,
        mesh=mesh,
        in_specs=(P("gx", "gy", None),),
        out_specs=(P("gx", "gy", None), P()),
        check_vma=False,
    )
```

time: 153 us -> 110 us (0.72)
  local copies, waits for them, and re-layouts: 26.3 us -> 4.31 us
  matrix products: 17.4 us -> 0 us
  other arithmetic: 12.4 us -> 0 us
  Pallas kernels: 93.1 us -> 104 us
  between operations: 2.56 us -> 0.64 us
    dot_general x18 -> x0, matrix products: 17.4 us -> none  [the longest x3 5.25 us: face(): part = jnp.einsum('fluq,vq->fluv', part, cheb_v, precision=HIGH)]
    slice x17 -> x0, local copies, waits for them, and re-layouts: 12 us -> none  [the longest x2 3.38 us: shards(): coef_hi[2]]
    pallas_call x3 -> x1, Pallas kernels: 93.1 us -> 104 us  [shards(): pl.pallas_call(functools.partial(kernel, p), in_specs=[anywhere] * (1 + l...]
    unnamed x56 -> x1, local copies, waits for them, and re-layouts: 12.1 us -> 3.13 us
    reduce_sum x6 -> x0, other arithmetic: 6.07 us -> none  [the longest x1 2.73 us: shards(): jnp.sum(tens * moments[:, 0], axis=3)]
    rsqrt x2 -> x0, other arithmetic: 2.11 us -> none  [face(): rinv = lax.rsqrt(0.25 + u[:, None] * u[:, None] + v[None, :] * v[None, :])]
where the time goes in v1:
time: 110 us; the launch traced here: 109 us
  Pallas kernels  104 us (95%)
  local copies, waits for them, and re-layouts  4.31 us (4%)
    pallas_call x1, Pallas kernels, shards(): pl.pallas_call(functools.partial(kernel, p), in_specs=[anywhere] * (1 + l...  104 us
    unnamed x1, local copies, waits for them, and re-layouts  3.13 us

profile of v1, /device:TPU:1, one launch (start us, length us, event | category | flops | bytes accessed | tf_op | source)
XLA Modules:
  0.0 109.4 jit_solution(1744656522174413330)
XLA Ops:
  0.6 104.4 %james.1 = (f32[32,64,256]{2,1,0:T(8,128)}, f32[8,128]{1,0:T(8,128)}) custom-call(f32[32,64,256]{2,1,0:T(8,128)} %rho_ref.1, bf16[2,256,256]{2,1,0:T(8,128)(2,1)} %constant.22.clone.refs_0_, f32[2,256,128]{2,1,0:T(8,128)} %constant.23.clone.refs_1_, f32[4,8,128]{2,1,0:T(8,128)} %constant.24.clone.refs_2_, bf16[2,32,256]{2,1,0:T(8,128)(2,1)} %constant.25.clone.refs_3_, ...), custom_call_target="tpu_custom_call" | custom-call | tf_op jit(solution)/shard_map/james/pallas_call | solution.py:852
  105.1 1.2 %slice_bitcast_fusion = f32[2]{0:T(128)} fusion(f32[8,128]{1,0:T(8,128)} %get-tuple-element.5), kind=kLoop, calls=%fused_computation | loop fusion | bytes 16 | tf_op jit(solution)/shard_map/squeeze | solution.py:863
  106.3 3.1 %copy.15 = f32[32,64,256]{2,1,0:T(8,128)} copy(f32[32,64,256]{2,1,0:T(8,128)} %get-tuple-element.8) | data formatting | bytes 4194304

commit v2 on v1

--- a/solution.py
+++ b/solution.py
@@ -22,6 +22,7 @@
 PER = LANES // BLOCK
 NBLK = -(-DEG // PER)
 MI = (DEG + 1) // 2
+LOT = 2 * PER * NBLK
 
 
 def solid_harmonics(x, y, z):
@@ -318,7 +319,7 @@
     return lax.broadcasted_iota(jnp.int32, shape, dim)
 
 
-def face_prep(p, dmat_ref, rx_ref, ra_ref):
+def face_prep(p, dmat_ref, r_ref):
     ix = lax.axis_index("gx")
     shape = (p.sub, LANES)
     cell = ix * p.ca + (iota(shape, 1) // p.kb) * p.sub + iota(shape, 0)
@@ -332,11 +333,13 @@
         u = (2 * (start + iota((rows, p.n), 0)) - (p.n - 1)).astype(jnp.float32) * (0.5 * p.h)
         v = (2 * iota((rows, p.n), 1) - (p.n - 1)).astype(jnp.float32) * (0.5 * p.h)
         return lax.rsqrt(0.25 + u * u + v * v)
-    rx_ref[...] = inverse_radius(p.n, 0)
-    ra_ref[...] = inverse_radius(p.ca, ix * p.ca)
-
-
-def moments(p, first_ref, rhs_ref, w_ref, v_ref, ktab_ref, dmat_ref, g_ref, y_ref, pay_ref):
+    r_ref[0:p.n] = inverse_radius(p.n, 0)
+    near = inverse_radius(p.ca, ix * p.ca)
+    for k in range(4):
+        r_ref[p.n + k * p.ca:p.n + (k + 1) * p.ca] = near
+
+
+def moments(p, first_ref, rhs_ref, w_ref, v_ref, ktab_ref, dmat_ref, g_ref, y_ref):
     ix, iy = lax.axis_index("gx"), lax.axis_index("gy")
     pair = 2 if p.sub % 2 == 0 else 1
     energy = jnp.zeros((8, LANES), jnp.float32)
@@ -373,9 +376,7 @@
     packed = y[0:ROWS]
     for i in range(1, 4):
         packed = jnp.where(which == i, y[i * ROWS:(i + 1) * ROWS], packed)
-    pay_ref[0:ROWS] = packed
-    pay_ref[ROWS:2 * ROWS] = mz
-    pay_ref[2 * ROWS:2 * ROWS + 8] = energy
+    return packed, mz, jnp.sum(energy, axis=1, keepdims=True)
 
 
 def sum_slots(ref, count):
@@ -421,7 +422,7 @@
     return jnp.where(odd, turn(x, 1), turn(x, -1))
 
 
-def coefficients(p, packed, mz, big_ref, sign_ref, gain_ref, same_ref, s_ref, coef_ref):
+def project(p, packed, mz, energy, big_ref, sign_ref, gain_ref, same_ref, s_ref):
     which = iota((ROWS, LANES), 1) // BLOCK
 
     def spread(x, i):
@@ -454,6 +455,8 @@
     hi, lo = split(s_ref[...].reshape(6 * NBLK * 16, LANES))
     spread_sum = (dot(hi, same_ref[...]) + dot(lo, same_ref[...])).reshape(3, 2, NBLK, 16, LANES)
     lane = iota((16, LANES), 1)
+    to = iota((8, LANES), 1)
+    pay = jnp.zeros((8, LANES), jnp.float32)
     for blk in range(NBLK):
         l = blk * PER + lane // BLOCK
         right = lane % 2 == 1
@@ -464,6 +467,31 @@
             wide = [jnp.where((lane + b) % 2 == 0, sz[a, blk], trade(sz[a, blk])) for a in range(2)]
             other = jnp.where((l + lane + b) % 2 == 1, wide[1], wide[0])
             lm.append((sx[b, blk] + jnp.where(cross, sy[1 - b, blk], sy[b, blk]) + other) * gain_ref[b, blk])
+        parts = [lm[0][:8], lm[1][:8], jnp.concatenate([lm[0][8:9], lm[1][8:9], jnp.zeros((6, LANES), jnp.float32)], axis=0)]
+        for part, x in enumerate(parts):
+            for i in range(PER):
+                at = part * LOT + 2 * (blk * PER + i)
+                pay = jnp.where((to >= at) & (to < at + 2), turn(x, at - i * BLOCK), pay)
+    return jnp.where(to == LANES - 1, energy, pay)
+
+
+def coefficients(p, total, big_ref, coef_ref):
+    to = iota((8, LANES), 1)
+    for blk in range(NBLK):
+        wide = []
+        for part in range(3):
+            x = jnp.zeros((8, LANES), jnp.float32)
+            for i in range(PER):
+                at = part * LOT + 2 * (blk * PER + i)
+                x = jnp.where((to >= i * BLOCK) & (to < i * BLOCK + 2), turn(total, i * BLOCK - at), x)
+            for shift in (2, 4, 8, 16):
+                x = x + turn(x, shift)
+            wide.append(x)
+        lm = [jnp.concatenate([wide[b], wide[2][b:b + 1], jnp.zeros((7, LANES), jnp.float32)], axis=0) for b in range(2)]
+        l = blk * PER + iota((16, LANES), 1) // BLOCK
+        lane = iota((16, LANES), 1)
+        right = lane % 2 == 1
+        cross = (l - lane) % 2 == 1
         rows = [lm, [jnp.where(cross, lm[1 - b], lm[b]) for b in range(2)],
                 [jnp.where(right, *[jnp.where((l + a) % 2 == 1, trade(lm[b]), lm[b]) for b in (1, 0)]) for a in range(2)]]
         cols = slice(blk * LANES, (blk + 1) * LANES)
@@ -501,36 +529,31 @@
     return jnp.where(iota(e.shape, 1) // BLOCK == 1, e - top, top).astype(BF16)
 
 
-def faces(p, c3_ref, cu_ref, vt_ref, rx_ref, ra_ref, fx_ref, fa_ref):
-    ix = lax.axis_index("gx")
-    edge = (ix == 0) | (ix == p.gx - 1)
-    fa_ref[...] = jnp.zeros_like(fa_ref)
-    near = pl.ds(pl.multiple_of(ix * p.ca, 16), p.ca)
-
-    @pl.when(edge)
-    def _():
-        fx_ref[...] = jnp.zeros_like(fx_ref)
-
-        def step(i, carry):
-            e = dot(cu_ref[...], c3_ref[DEG - 1 - i, 0])
-            fx_ref[...] = fx_ref[...] * rx_ref[...] + dot(triple(e), vt_ref[...])
-            return carry
-
-        lax.fori_loop(0, DEG, step, 0)
-
-    def step(i, carry):
-        e = dot(cu_ref[near], jnp.concatenate([c3_ref[DEG - 1 - i, k] for k in range(1, 5)], axis=1))
+def faces(p, c3_ref, cu_ref, vt_ref, r_ref, e_ref, f_ref):
+    near = pl.ds(pl.multiple_of(lax.axis_index("gx") * p.ca, 16), p.ca)
+    rows = p.n + 4 * p.ca
+    for l in range(DEG):
+        e_ref[l, 0:p.n] = triple(dot(cu_ref[...], c3_ref[l, 0]))
+        e = dot(cu_ref[near], jnp.concatenate([c3_ref[l, k] for k in range(1, 5)], axis=1))
         e = jnp.concatenate([e[:, k * LANES:(k + 1) * LANES] for k in range(4)], axis=0)
-        ra = jnp.concatenate([ra_ref[...]] * 4, axis=0)
-        fa_ref[...] = fa_ref[...] * ra + dot(triple(e), vt_ref[...])
+        e_ref[l, p.n:rows] = triple(e)
+    tile = 64
+
+    def step(t, carry):
+        at = pl.ds(pl.multiple_of(t * tile, tile), tile)
+        r = r_ref[at]
+        acc = dot(e_ref[DEG - 1, at], vt_ref[...])
+        for l in range(DEG - 2, -1, -1):
+            acc = acc * r + dot(e_ref[l, at], vt_ref[...])
+        f_ref[at] = acc
         return carry
 
-    lax.fori_loop(0, DEG, step, 0)
-
-
-def add_faces(p, rhs_ref, sine_ref, jtab_ref, ktab_ref, fx_ref, fa_ref):
+    lax.fori_loop(0, rows // tile, step, 0)
+
+
+def add_faces(p, rhs_ref, sine_ref, jtab_ref, ktab_ref, f_ref):
     ix, iy = lax.axis_index("gx"), lax.axis_index("gy")
-    ca = p.ca
+    ca, n = p.ca, p.n
     chunk = pl.ds(pl.multiple_of(iy * p.kb, 16), p.kb)
     near = [jnp.concatenate([sine_ref[i, chunk]] * p.pack, axis=0) for i in range(2)]
 
@@ -540,12 +563,12 @@
 
     @pl.when((ix == 0) | (ix == p.gx - 1))
     def _():
-        hat = left_mul(sine_ref, to_lanes(fx_ref[...]))
+        hat = left_mul(sine_ref, to_lanes(f_ref[0:n]))
         place = p.lanes(p.n)
         rhs_ref[0] += jnp.where((place == 0) & (ix == 0), hat, 0.0)
         rhs_ref[p.sub - 1] += jnp.where((place == p.pack - 1) & (ix == p.gx - 1), hat, 0.0)
 
-    hy = to_lanes(fa_ref[0:2 * ca])
+    hy = to_lanes(f_ref[n:n + 2 * ca])
     place = p.lanes(p.sub)
     planes = []
     for f in range(2):
@@ -555,7 +578,7 @@
         planes.append(acc)
     plus, minus = planes[0] + planes[1], planes[0] - planes[1]
 
-    hi, lo = split(jnp.concatenate([fa_ref[2 * ca:4 * ca]] * (LANES // (2 * ca)), axis=0))
+    hi, lo = split(jnp.concatenate([f_ref[n + 2 * ca:n + 4 * ca]] * (LANES // (2 * ca)), axis=0))
     hz = dot_t(sine_ref[0], hi) + dot_t(sine_ref[1], hi) + dot_t(sine_ref[0], lo)
     top = hz.astype(BF16).astype(jnp.float32)
     both = jnp.where(iota(hz.shape, 1) // (2 * ca) == 1, hz - top, top).astype(BF16)
@@ -588,8 +611,8 @@
     local = rest[:len(names)]
     (x_ref, send_ref, spec_ref, rhs_ref, first_ref, tab_ref, left_ref, right_ref, edge_ref, carry_ref,
      got_ref, back_ref, ends_ref, got2_ref, back2_ref, ends2_ref,
-     dmat_ref, rx_ref, ra_ref, g_ref, y_ref, pay_ref, pxs_ref, psum_ref, pys_ref,
-     s_ref, coef_ref, c3_ref, fx_ref, fa_ref,
+     dmat_ref, r_ref, g_ref, y_ref, pay_ref, pxs_ref, psum_ref, pys_ref,
+     s_ref, coef_ref, c3_ref, e_ref, f_ref,
      part_ref, xs_ref, sum_ref, ys_ref, u_ref, res_ref, fin_ref,
      table_sems, in_sems, out_sems, land_sems, back_out_sems, back_land_sems,
      line_sems, line2_sems, pay_sems, sum_sems, write_sems) = rest[len(names):]
@@ -650,7 +673,7 @@
     mode_tables(p, jtab_ref, ktab_ref, tab_ref)
     for d in order:
         swap(p.chunks - 1, d).start()
-    face_prep(p, dmat_ref, rx_ref, ra_ref)
+    face_prep(p, dmat_ref, r_ref)
 
     def across(c, carry):
         for d in order:
@@ -688,13 +711,14 @@
     for copy in staged[3:]:
         copy.wait()
 
-    moments(p, first_ref, rhs_ref, wide_ref, lanes_ref, ktab_ref, dmat_ref, g_ref, y_ref, pay_ref)
+    sums = moments(p, first_ref, rhs_ref, wide_ref, lanes_ref, ktab_ref, dmat_ref, g_ref, y_ref)
+    pay_ref[...] = project(p, *sums, big_ref, sign_ref, gain_ref, same_ref, s_ref)
     total = all_sum(p, pay_ref, pxs_ref, psum_ref, pys_ref, pay_sems)
-    energy_one = jnp.sum(total[2 * ROWS:2 * ROWS + 8])
-    coefficients(p, total[:ROWS], total[ROWS:2 * ROWS], big_ref, sign_ref, gain_ref, same_ref, s_ref, coef_ref)
+    energy_one = jnp.sum(jnp.where(iota(total.shape, 1) == LANES - 1, total, 0.0))
+    coefficients(p, total, big_ref, coef_ref)
     face_coefs(p, coef_ref, sign_ref, c3_ref)
-    faces(p, c3_ref, cu_ref, vt_ref, rx_ref, ra_ref, fx_ref, fa_ref)
-    add_faces(p, rhs_ref, sine_ref, jtab_ref, ktab_ref, fx_ref, fa_ref)
+    faces(p, c3_ref, cu_ref, vt_ref, r_ref, e_ref, f_ref)
+    add_faces(p, rhs_ref, sine_ref, jtab_ref, ktab_ref, f_ref)
 
     edge_sums(p, rhs_ref, tab_ref, left_ref, right_ref, edge_ref)
     ea = total_copies(p, part_ref, xs_ref, sum_sems, "gx", 0)
@@ -830,7 +854,7 @@
     cube = (p.sub, p.n, LANES)
     plane = (p.n, LANES)
     slots = (p.gx, p.jb, LANES)
-    pay = (2 * ROWS + 8, LANES)
+    pay = (8, LANES)
     box = (p.gy, p.sub, p.cb, LANES)
     vmem = lambda shape, dtype=f32: pltpu.VMEM(shape, dtype)
     dma = pltpu.SemaphoreType.DMA
@@ -840,10 +864,10 @@
     scratch += [vmem(whole), vmem(box), vmem(cube), vmem(cube), vmem(cube), vmem((6,) + plane)]
     scratch += [vmem(plane)] * 4
     scratch += [vmem(slots), vmem(slots), vmem(plane)] * 2
-    scratch += [vmem((DEG, p.sub, LANES)), vmem((p.n, p.n)), vmem((p.ca, p.n)), vmem((p.sub, ROWS + 8, LANES)),
+    scratch += [vmem((DEG, p.sub, LANES)), vmem((p.n + 4 * p.ca, p.n)), vmem((p.sub, ROWS + 8, LANES)),
                 vmem((2 * ROWS, LANES)), vmem(pay), vmem((p.gx,) + pay), vmem(pay), vmem((p.gy,) + pay)]
     scratch += [vmem((3, 2, NBLK, 16, LANES)), vmem((3, NBLK, ROWS, LANES)), vmem((DEG, 5, LANES, LANES), BF16),
-                vmem((p.n, p.n)), vmem((4 * p.ca, p.n))]
+                vmem((DEG, p.n + 4 * p.ca, LANES), BF16), vmem((p.n + 4 * p.ca, p.n))]
     scratch += [vmem((8, LANES)), vmem((p.gx, 8, LANES)), vmem((8, LANES)), vmem((p.gy, 8, LANES)),
                 vmem(cube), vmem(box), vmem(whole)]
     most = max(p.gx, p.gy)

time: 110 us -> 99.2 us (0.902)
  Pallas kernels: 104 us -> 94 us
    pallas_call x1, Pallas kernels: 104 us -> 94 us  [shards(): pl.pallas_call(functools.partial(kernel, p), in_specs=[anywhere] * (1 + l...]
where the time goes in v2:
time: 99.2 us; the launch traced here: 99 us
  Pallas kernels  94 us (95%)
  local copies, waits for them, and re-layouts  4.31 us (4%)
    pallas_call x1, Pallas kernels, shards(): pl.pallas_call(functools.partial(kernel, p), in_specs=[anywhere] * (1 + l...  94 us
    unnamed x1, local copies, waits for them, and re-layouts  3.13 us

profile of v2, /device:TPU:1, one launch (start us, length us, event | category | flops | bytes accessed | tf_op | source)
XLA Modules:
  0.0 99.0 jit_solution(893408574333581979)
XLA Ops:
  0.6 94.0 %james.1 = (f32[32,64,256]{2,1,0:T(8,128)}, f32[8,128]{1,0:T(8,128)}) custom-call(f32[32,64,256]{2,1,0:T(8,128)} %rho_ref.1, bf16[2,256,256]{2,1,0:T(8,128)(2,1)} %constant.22.clone.refs_0_, f32[2,256,128]{2,1,0:T(8,128)} %constant.23.clone.refs_1_, f32[4,8,128]{2,1,0:T(8,128)} %constant.24.clone.refs_2_, bf16[2,32,256]{2,1,0:T(8,128)(2,1)} %constant.25.clone.refs_3_, ...), custom_call_target="tpu_custom_call" | custom-call | tf_op jit(solution)/shard_map/james/pallas_call | solution.py:876
  94.7 1.2 %slice_bitcast_fusion = f32[2]{0:T(128)} fusion(f32[8,128]{1,0:T(8,128)} %get-tuple-element.5), kind=kLoop, calls=%fused_computation | loop fusion | bytes 16 | tf_op jit(solution)/shard_map/squeeze | solution.py:887
  95.9 3.1 %copy.15 = f32[32,64,256]{2,1,0:T(8,128)} copy(f32[32,64,256]{2,1,0:T(8,128)} %get-tuple-element.8) | data formatting | bytes 4194304

commit v3 on v2

--- a/solution.py
+++ b/solution.py
@@ -238,7 +238,6 @@
     deg = row_degrees()
     weights = expansion_weights() * (RADIUS ** -np.arange(DEG, dtype=np.float64))[:, None] * (p.norm / p.h)
     big = np.zeros((3, MI, ROWS, NBLK * LANES))
-    sign = np.ones((3, ROWS, NBLK * LANES))
     gain = np.zeros((2, NBLK, 16, LANES))
     for l in range(DEG):
         for face in range(3):
@@ -256,7 +255,6 @@
                         odd = q % 2
                         mpar = (r + odd) % 2
                     at = l * BLOCK + q
-                    sign[face, i, at] = (-1.0) ** (mpar + odd, odd, l + mpar)[face]
                     for mi in range(MI):
                         m = mpar + 2 * mi
                         if m <= l and not (odd and m == 0):
@@ -268,7 +266,7 @@
                     if m <= l:
                         at = (l % PER) * BLOCK + c
                         gain[odd, l // PER, mi, at : (l % PER + 1) * BLOCK : 2] = weights[l, m]
-    return big.astype(np.float32), sign.astype(np.float32), gain.astype(np.float32)
+    return big.astype(np.float32), gain.astype(np.float32)
 
 
 def tables(p):
@@ -298,8 +296,20 @@
     ch, cl = split_table(cols)
     same = np.arange(LANES)
     same = (same[:, None] // BLOCK == same[None, :] // BLOCK) & ((same[:, None] - same[None, :]) % 2 == 0)
-    big, sign, gain = harmonic_tables(p)
+    big, gain = harmonic_tables(p)
     f32 = np.float32
+    own = np.arange(p.cb) + 1
+    small = np.sin(np.pi * ((own[:, None] * own[None, :]) % (2 * (p.cb + 1))) / (p.cb + 1))
+    small_eps = 4.0 * np.sin(np.pi * own / (2.0 * (p.cb + 1))) ** 2
+    ltab = np.stack([np.repeat(v[:, None], LANES, axis=1) for v in (small_eps, small[0])])
+    rtab = np.zeros((8, n))
+    rtab[0], rtab[1] = eps, sine[0]
+    pick = np.zeros((max(16, 2 * p.gy), n))
+    for q in range(p.gy):
+        if q > 0:
+            pick[2 * q] = sine[q * p.cb - 1]
+        if q < p.gy - 1:
+            pick[2 * q + 1] = sine[(q + 1) * p.cb]
     return [
         np.stack(split_table(sine)),
         jtab.astype(f32),
@@ -309,9 +319,12 @@
         np.concatenate([rh, rl, rh, np.zeros_like(rh)], axis=1),
         np.concatenate([ch, ch, cl, np.zeros_like(ch)], axis=0),
         big,
-        sign,
         gain,
         same.astype(BF16),
+        np.stack(split_table(np.tile(small, (1, n // p.cb)))),
+        ltab.astype(f32),
+        rtab.astype(f32),
+        np.stack(split_table(pick)),
     ]
 
 
@@ -417,12 +430,19 @@
     return sum_slots(ys_ref, p.gy)
 
 
+def mirror(blk):
+    shape = (ROWS, LANES)
+    lane = iota(shape, 1)
+    total = blk * PER + lane // BLOCK + lane + (iota(shape, 0) >= EVEN).astype(jnp.int32)
+    return jnp.where(total % 2 == 0, 1.0, -1.0)
+
+
 def trade(x):
     odd = iota(x.shape, 1) % 2 == 1
     return jnp.where(odd, turn(x, 1), turn(x, -1))
 
 
-def project(p, packed, mz, energy, big_ref, sign_ref, gain_ref, same_ref, s_ref):
+def project(p, packed, mz, energy, big_ref, gain_ref, same_ref, s_ref):
     which = iota((ROWS, LANES), 1) // BLOCK
 
     def spread(x, i):
@@ -447,7 +467,7 @@
         lo, hi = pairs[face]
         for blk in range(NBLK):
             cols = slice(blk * LANES, (blk + 1) * LANES)
-            both = hi + sign_ref[face][:, cols] * lo
+            both = hi + mirror(blk) * lo
             for mi in range(MI):
                 prod = big_ref[face, mi][:, cols] * both
                 s_ref[face, 0, blk, mi:mi + 1] = jnp.sum(prod[:EVEN], axis=0, keepdims=True)
@@ -505,17 +525,16 @@
             coef_ref[face, blk] = jnp.concatenate([even, odd], axis=0)
 
 
-def face_coefs(p, coef_ref, sign_ref, c3_ref):
+def face_coefs(p, coef_ref, c3_ref):
     ix = lax.axis_index("gx")
     which = iota((ROWS, LANES), 1) // BLOCK
     gap = jnp.zeros((BLOCK - ROWS, LANES), jnp.float32)
     rest = jnp.zeros((LANES - 3 * BLOCK, LANES), jnp.float32)
     for l in range(DEG):
         blk, i = divmod(l, PER)
-        cols = slice(blk * LANES, (blk + 1) * LANES)
         for face in range(3):
             hi = coef_ref[face, blk]
-            lo = hi * sign_ref[face][:, cols]
+            lo = hi * mirror(blk)
             for k, c in enumerate([jnp.where(ix == 0, lo, hi)] if face == 0 else [lo, hi]):
                 c = turn(jnp.where(which == i, c, 0.0), -i * BLOCK)
                 c = c + turn(c, BLOCK) + turn(c, 2 * BLOCK)
@@ -603,21 +622,126 @@
             rhs_ref[at] += add[:, e * LANES:(e + 1) * LANES] + jtab_ref[1] * wave
 
 
+def wide(p, x):
+    return jnp.concatenate([x] * (p.n // LANES), axis=1)
+
+
+def local_prep(p, loc_ref, ltab_ref, rtab_ref, z_ref, kron_ref, lmode_ref, t_ref):
+    sigma = wide(p, ltab_ref[0]) + rtab_ref[0:1]
+    s = 0.5 * jnp.sqrt(sigma)
+    t = jnp.sqrt(1.0 + s * s)
+    theta = 2.0 * jnp.log1p(s + s * s / (1.0 + t))
+    lam = jnp.exp(-theta)
+    last = float(p.ca + 1)
+    lmode_ref[0] = lam
+    lmode_ref[1] = (4.0 * p.h**3 / (p.cb + 1)) / (4.0 * s * t)
+    lmode_ref[2] = jnp.exp(-theta * last)
+    lmode_ref[3] = lam / (1.0 - jnp.exp(-theta * (2.0 * last)))
+    block = iota((p.cb, p.n), 1) // p.cb
+    for i in range(2):
+        tile = loc_ref[i].astype(jnp.float32)
+        for b in range(p.n // p.cb):
+            kron_ref[i, b * p.cb:(b + 1) * p.cb] = jnp.where(block == b, tile, 0.0).astype(BF16)
+
+    def step(c, carry):
+        rows = pl.ds(c * p.gy, p.gy)
+        t_ref[rows] = left_mul(kron_ref, z_ref[rows].reshape(p.n, p.n)).reshape(p.gy, p.cb, p.n)
+        return carry
+
+    lax.fori_loop(0, p.ca // p.gy, step, 0)
+
+
+def local_sources(p, f_ref, sine_ref, kron_ref, rtab_ref, t_ref, yb_ref, xb_ref):
+    ix, iy = lax.axis_index("gx"), lax.axis_index("gy")
+    ca, n = p.ca, p.n
+    own = pl.ds(pl.multiple_of(iy * p.cb, 16), p.cb)
+    hi, lo = split(jnp.concatenate([f_ref[n + 2 * ca:n + 4 * ca]] * (LANES // (2 * ca)), axis=0))
+    hz = dot_t(kron_ref[0, own], hi) + dot_t(kron_ref[1, own], hi) + dot_t(kron_ref[0, own], lo)
+    other = turn(hz, -ca)
+    plus, minus = hz + other, hz - other
+    even = iota((p.cb, n), 1) % 2 == 0
+    for x in range(ca):
+        t_ref[x] += rtab_ref[1:2] * jnp.where(even, plus[:, x:x + 1], minus[:, x:x + 1])
+    hat = right_mul(f_ref[n:n + 2 * ca], sine_ref)
+    yb_ref[0] = jnp.where(iy == 0, hat[:ca], 0.0)
+    yb_ref[1] = jnp.where(iy == p.gy - 1, hat[ca:], 0.0)
+    hat = right_mul(f_ref[own], sine_ref)
+    xb_ref[0] = jnp.where(ix == 0, hat, 0.0)
+    xb_ref[1] = jnp.where(ix == p.gx - 1, hat, 0.0)
+
+
+def gather_lanes(p, parts, g):
+    place = p.lanes(parts[0].shape[0])
+    per = LANES // p.kb
+    cols = []
+    for col in range(p.n // LANES):
+        acc = None
+        for e in range(per):
+            part = turn(parts[col * per + e], (e - g) * p.kb)
+            acc = part if acc is None else jnp.where(place == e, part, acc)
+        cols.append(acc)
+    return jnp.concatenate(cols, axis=1)
+
+
+def local_solve(p, xgot_ref, ygot_ref, xb_ref, yb_ref, ltab_ref, lmode_ref, kron_ref, wave_ref, t_ref, z_ref):
+    ca, cb, n = p.ca, p.cb, p.n
+    sides = [gather_lanes(p, [xgot_ref[q] for q in range(p.gy)], g) + xb_ref[e] for e, g in ((0, 0), (1, p.pack - 1))]
+    if n > 2 * cb:
+        sides.append(jnp.zeros((n - 2 * cb, n), jnp.float32))
+    hat = left_mul(kron_ref, jnp.concatenate(sides, axis=0))
+    t_ref[0] += hat[:cb]
+    t_ref[ca - 1] += hat[cb:2 * cb]
+    rows = []
+    for e in range(2):
+        got = [gather_lanes(p, [ygot_ref[q, e] for q in range(p.gy)], g) for g in range(p.pack)]
+        rows.append(jnp.concatenate(got, axis=0) + yb_ref[e])
+    wave_ref[0] = rows[0] + rows[1]
+    wave_ref[1] = rows[0] - rows[1]
+    tile = 16
+
+    def strip(j, carry):
+        at = pl.ds(pl.multiple_of(j * tile, tile), tile)
+        lam, inv = lmode_ref[0, at], lmode_ref[1, at]
+        column = wide(p, ltab_ref[1, at])
+        even = iota((tile, n), 0) % 2 == 0
+        left = jnp.zeros((tile, n), jnp.float32)
+        for i in range(ca):
+            v = t_ref[i, at] + column * jnp.where(even, wave_ref[0, i:i + 1], wave_ref[1, i:i + 1])
+            t_ref[i, at] = v
+            left = left * lam + v
+        right = t_ref[ca - 1, at]
+        for i in range(ca - 2, -1, -1):
+            right = right * lam + t_ref[i, at]
+        f0, f1 = right * lmode_ref[3, at], left * lmode_ref[3, at]
+        a = f1 * lmode_ref[2, at] - f0
+        b = f0 * lmode_ref[2, at] - f1
+        for i in range(ca - 1, -1, -1):
+            b = b * lam
+            z_ref[i, at] = b
+            b = b + t_ref[i, at]
+        for i in range(ca):
+            a = a * lam + t_ref[i, at]
+            z_ref[i, at] = (a + z_ref[i, at]) * inv
+        return carry
+
+    lax.fori_loop(0, cb // tile, strip, 0)
+
+
 def kernel(p, rho_ref, *refs):
-    names = ("sine", "jtab", "ktab", "wide", "lanes", "cu", "vt", "big", "sign", "gain", "same")
+    names = ("sine", "jtab", "ktab", "wide", "lanes", "cu", "vt", "big", "gain", "same", "loc", "ltab", "rtab", "pick")
     hbm = refs[:len(names)]
     out_ref, energy_ref = refs[len(names):len(names) + 2]
     rest = refs[len(names) + 2:]
     local = rest[:len(names)]
-    (x_ref, send_ref, spec_ref, rhs_ref, first_ref, tab_ref, left_ref, right_ref, edge_ref, carry_ref,
+    (x_ref, send_ref, spec_ref, rhs_ref, first_ref, tab_ref, left_ref, right_ref, edge_ref, wall_ref,
      got_ref, back_ref, ends_ref, got2_ref, back2_ref, ends2_ref,
      dmat_ref, r_ref, g_ref, y_ref, pay_ref, pxs_ref, psum_ref, pys_ref,
      s_ref, coef_ref, c3_ref, e_ref, f_ref,
-     part_ref, xs_ref, sum_ref, ys_ref, u_ref, res_ref, fin_ref,
-     table_sems, in_sems, out_sems, land_sems, back_out_sems, back_land_sems,
+     part_ref, xs_ref, sum_ref, ys_ref, fin_ref, z_ref, t_ref, kron_ref, lmode_ref,
+     xg_ref, xgot_ref, yg_ref, ygot_ref, yb_ref, xb_ref, wave_ref,
+     table_sems, in_sems, out_sems, land_sems, ghost_out_sems, ghost_land_sems,
      line_sems, line2_sems, pay_sems, sum_sems, write_sems) = rest[len(names):]
-    sine_ref, jtab_ref, ktab_ref, wide_ref, lanes_ref, cu_ref, vt_ref, big_ref, sign_ref, gain_ref, same_ref = local
-    w_ref = spec_ref
+    sine_ref, jtab_ref, ktab_ref, wide_ref, lanes_ref, cu_ref, vt_ref, big_ref, gain_ref, same_ref, loc_ref, ltab_ref, rtab_ref, pick_ref = local
     ix, iy = lax.axis_index("gx"), lax.axis_index("gy")
     order = list(range(p.gy // 2, p.gy)) + list(range(1, p.gy // 2))
     block = p.step * p.cb
@@ -649,6 +773,8 @@
             [x_ref[pl.ds(g * p.sub + c * p.step, p.step)].reshape(block, p.n) for g in range(p.pack)], axis=0
         )
         y = right_mul(x, sine_ref)
+        for g in range(p.pack):
+            z_ref[pl.ds(g * p.sub + c * p.step, p.step)] = y[g * block:(g + 1) * block].reshape(p.step, p.cb, p.n)
         place = p.lanes(block)
         planes = pl.ds(c * p.step, p.step)
         for q in range(p.gy):
@@ -674,6 +800,9 @@
     for d in order:
         swap(p.chunks - 1, d).start()
     face_prep(p, dmat_ref, r_ref)
+    for copy in staged[3:]:
+        copy.wait()
+    local_prep(p, loc_ref, ltab_ref, rtab_ref, z_ref, kron_ref, lmode_ref, t_ref)
 
     def across(c, carry):
         for d in order:
@@ -708,15 +837,12 @@
         return carry
 
     lax.fori_loop(0, p.chunks, drain, 0)
-    for copy in staged[3:]:
-        copy.wait()
-
     sums = moments(p, first_ref, rhs_ref, wide_ref, lanes_ref, ktab_ref, dmat_ref, g_ref, y_ref)
-    pay_ref[...] = project(p, *sums, big_ref, sign_ref, gain_ref, same_ref, s_ref)
+    pay_ref[...] = project(p, *sums, big_ref, gain_ref, same_ref, s_ref)
     total = all_sum(p, pay_ref, pxs_ref, psum_ref, pys_ref, pay_sems)
     energy_one = jnp.sum(jnp.where(iota(total.shape, 1) == LANES - 1, total, 0.0))
     coefficients(p, total, big_ref, coef_ref)
-    face_coefs(p, coef_ref, sign_ref, c3_ref)
+    face_coefs(p, coef_ref, c3_ref)
     faces(p, c3_ref, cu_ref, vt_ref, r_ref, e_ref, f_ref)
     add_faces(p, rhs_ref, sine_ref, jtab_ref, ktab_ref, f_ref)
 
@@ -733,6 +859,7 @@
                     energy = energy + prod[r * 8:(r + 1) * 8]
             part_ref[...] = energy
             xs_ref[ix] = energy
+            local_sources(p, f_ref, sine_ref, kron_ref, rtab_ref, t_ref, yb_ref, xb_ref)
             return
         for c in ea:
             c.start()
@@ -740,110 +867,84 @@
     line_exchange(p, tab_ref, edge_ref, got2_ref, back2_ref, ends2_ref, line2_sems, between)
     for t in range(p.n // p.tile):
         rows = pl.ds(t * p.tile, p.tile)
-        lam = tab_ref[0, rows]
+        lam, inv = tab_ref[0, rows], tab_ref[1, rows] * (2.0 / p.h)
         a, b = carries(p, rows, tab_ref, left_ref, right_ref, ends2_ref)
-        carry_ref[rows] = a
+        low, high = a, b
         for i in range(p.sub - 1, -1, -1):
             b = b * lam
             first_ref[i, rows] = b
             b = b + rhs_ref[i, rows]
+        low = low + b * lam
+        for i in range(p.sub):
+            a = a * lam + rhs_ref[i, rows]
+            first_ref[i, rows] = (a + first_ref[i, rows]) * inv
+        high = high + a * lam
+        wall_ref[rows] = jnp.where(p.lanes(p.tile) == 0, low, high) * inv
+    xg_ref[...] = left_mul(sine_ref, wall_ref[...])
+
+    def ghost(k, d):
+        q = lax.rem(iy + d, p.gy)
+        src = yg_ref.at[q] if k else xg_ref.at[pl.ds(q * p.cb, p.cb)]
+        dst = ygot_ref if k else xgot_ref
+        return remote(src, dst.at[iy], ghost_out_sems.at[k, d], ghost_land_sems.at[k, d], {"gy": q})
+
+    pair = 2 if p.sub % 2 == 0 else 1
+    for s in range(0, p.sub, pair):
+        y = left_mul(pick_ref, jnp.concatenate([first_ref[s + e] for e in range(pair)], axis=1))
+        if s == 0:
+            for d in order:
+                ghost(0, d).start()
+        for e in range(pair):
+            for q in range(p.gy):
+                for f in range(2):
+                    yg_ref[q, f, s + e:s + e + 1] = y[2 * q + f:2 * q + f + 1, e * LANES:(e + 1) * LANES]
+    xgot_ref[iy] = xg_ref[pl.ds(pl.multiple_of(iy * p.cb, 16), p.cb)]
+    ygot_ref[iy] = yg_ref[iy]
+    for d in order:
+        ghost(1, d).start()
     for c in ea:
         c.wait_recv()
     total = sum_slots(xs_ref, p.gx)
     sum_ref[...] = total
     ys_ref[iy] = total
 
-    def swap_back(c, d):
-        q = lax.rem(iy + d, p.gy)
-        planes = pl.ds(c * p.step, p.step)
-        return remote(u_ref.at[planes, pl.ds(q * p.cb, p.cb)], res_ref.at[iy, planes],
-                      back_out_sems.at[c, d], back_land_sems.at[c, d], {"gy": q})
-
-    def back_across(c, carry):
-        for t in range(p.n // p.tile):
-            rows = pl.ds(t * p.tile, p.tile)
-            lam, inv = tab_ref[0, rows], tab_ref[1, rows] * p.norm
-            a = carry_ref[rows]
-            for i in range(p.step):
-                s = c * p.step + i
-                a = a * lam + rhs_ref[s, rows]
-                first_ref[s, rows] = (a + first_ref[s, rows]) * inv
-            carry_ref[rows] = a
-        for i in range(0, p.step, p.pair):
-            s = c * p.step + i
-            x = jnp.concatenate([first_ref[s + e] for e in range(p.pair)], axis=1)
-            y = left_mul(sine_ref, x)
-            for e in range(p.pair):
-                u_ref[s + e] = y[:, e * LANES:(e + 1) * LANES]
-        planes = pl.ds(c * p.step, p.step)
-
-        @pl.when(c > 0)
-        def _():
-            for d in order:
-                swap_back(c - 1, d).start()
-
-        res_ref[iy, planes] = u_ref[planes, pl.ds(iy * p.cb, p.cb)]
-        return carry
-
-    lax.fori_loop(0, p.chunks, back_across, 0)
     for c in eb:
         c.start()
     for d in order:
-        swap_back(p.chunks - 1, d).start()
-
-    def write(c, g):
-        rows = pl.ds(g * p.sub + c * p.step, p.step)
-        return pltpu.make_async_copy(fin_ref.at[rows], out_ref.at[rows], write_sems.at[c, g])
+        for k in range(2):
+            ghost(k, d).wait_recv()
+    local_solve(p, xgot_ref, ygot_ref, xb_ref, yb_ref, ltab_ref, lmode_ref, kron_ref, wave_ref, t_ref, z_ref)
+
+    def write(c):
+        rows = pl.ds(c * p.gy, p.gy)
+        return pltpu.make_async_copy(fin_ref.at[rows], out_ref.at[rows], write_sems.at[c])
 
     def finish(c, carry):
-        for d in order:
-            swap_back(c, d).wait_recv()
-        planes = pl.ds(c * p.step, p.step)
-        place = p.lanes(block)
-        parts = [res_ref[q, planes].reshape(block, LANES) for q in range(p.gy)]
-        per = LANES // p.kb
-        rows = []
-        for g in range(p.pack):
-            cols = []
-            for col in range(p.n // LANES):
-                acc = None
-                for e in range(per):
-                    part = turn(parts[col * per + e], (e - g) * p.kb)
-                    acc = part if acc is None else jnp.where(place == e, part, acc)
-                cols.append(acc)
-            rows.append(jnp.concatenate(cols, axis=1))
-        y = right_mul(jnp.concatenate(rows, axis=0), sine_ref)
-        for g in range(p.pack):
-            at = pl.ds(g * p.sub + c * p.step, p.step)
-            fin_ref[at] = y[g * block:(g + 1) * block].reshape(p.step, p.cb, p.n)
+        rows = pl.ds(c * p.gy, p.gy)
+        y = right_mul(left_mul(kron_ref, z_ref[rows].reshape(p.n, p.n)), sine_ref)
+        fin_ref[rows] = y.reshape(p.gy, p.cb, p.n)
 
         @pl.when(c > 0)
         def _():
-            for g in range(p.pack):
-                write(c - 1, g).start()
+            write(c - 1).start()
 
         return carry
 
-    lax.fori_loop(0, p.chunks, finish, 0)
+    groups = p.ca // p.gy
+    lax.fori_loop(0, groups, finish, 0)
     for c in eb:
         c.wait_recv()
     energy_two = jnp.sum(sum_slots(ys_ref, p.gy))
-    for g in range(p.pack):
-        write(p.chunks - 1, g).start()
+    write(groups - 1).start()
     scale = p.h**3 * p.norm
     energy_ref[...] = jnp.where(iota((8, LANES), 1) == 0, energy_one, energy_two) * scale
-    for c in range(p.chunks):
-        for g in range(p.pack):
-            write(c, g).wait()
+    for c in range(groups):
+        write(c).wait()
     for c in ea + eb:
         c.wait_send()
-
-    def back_drain(c, carry):
-        for d in order:
-            swap_back(c, d).wait_send()
-        return carry
-
-    lax.fori_loop(0, p.chunks, back_drain, 0)
+    for d in order:
+        for k in range(2):
+            ghost(k, d).wait_send()
 
 
 def shards(charge_density):
@@ -869,10 +970,12 @@
     scratch += [vmem((3, 2, NBLK, 16, LANES)), vmem((3, NBLK, ROWS, LANES)), vmem((DEG, 5, LANES, LANES), BF16),
                 vmem((DEG, p.n + 4 * p.ca, LANES), BF16), vmem((p.n + 4 * p.ca, p.n))]
     scratch += [vmem((8, LANES)), vmem((p.gx, 8, LANES)), vmem((8, LANES)), vmem((p.gy, 8, LANES)),
-                vmem(cube), vmem(box), vmem(whole)]
+                vmem(whole), vmem(whole), vmem(whole), vmem((2, n, n), BF16), vmem((4, cb, n)),
+                vmem(plane), vmem((p.gy, cb, LANES)), vmem((p.gy, 2, p.sub, LANES)), vmem((p.gy, 2, p.sub, LANES)),
+                vmem((2, ca, n)), vmem((2, cb, n)), vmem((2, ca, n))]
     most = max(p.gx, p.gy)
-    scratch += [dma((len(data),)), dma((p.chunks, p.pack))] + [dma((p.chunks, p.gy))] * 4
-    scratch += [dma((4, p.gx))] * 2 + [dma((4, most))] * 2 + [dma((p.chunks, p.pack))]
+    scratch += [dma((len(data),)), dma((p.chunks, p.pack))] + [dma((p.chunks, p.gy))] * 2 + [dma((2, p.gy))] * 2
+    scratch += [dma((4, p.gx))] * 2 + [dma((4, most))] * 2 + [dma((p.ca // p.gy,))]
     potential, energies = pl.pallas_call(
         functools.partial(kernel, p),
         in_specs=[anywhere] * (1 + len(data)),

time: 99.2 us -> 85.3 us (0.86)
  Pallas kernels: 94 us -> 79.7 us
    pallas_call x1, Pallas kernels: 94 us -> 79.7 us  [shards(): pl.pallas_call(functools.partial(kernel, p), in_specs=[anywhere] * (1 + l...]
where the time goes in v3:
time: 85.3 us; the launch traced here: 84.7 us
  Pallas kernels  79.7 us (93%)
  local copies, waits for them, and re-layouts  4.31 us (5%)
    pallas_call x1, Pallas kernels, shards(): pl.pallas_call(functools.partial(kernel, p), in_specs=[anywhere] * (1 + l...  79.7 us
    unnamed x1, local copies, waits for them, and re-layouts  3.13 us

profile of v3, /device:TPU:1, one launch (start us, length us, event | category | flops | bytes accessed | tf_op | source)
XLA Modules:
  0.0 84.7 jit_solution(4698459048991005255)
XLA Ops:
  0.6 79.7 %james.1 = (f32[32,64,256]{2,1,0:T(8,128)}, f32[8,128]{1,0:T(8,128)}) custom-call(f32[32,64,256]{2,1,0:T(8,128)} %rho_ref.1, bf16[2,256,256]{2,1,0:T(8,128)(2,1)} %constant.28.clone.refs_0_, f32[2,256,128]{2,1,0:T(8,128)} %constant.29.clone.refs_1_, f32[4,8,128]{2,1,0:T(8,128)} %constant.30.clone.refs_2_, bf16[2,32,256]{2,1,0:T(8,128)(2,1)} %constant.31.clone.refs_3_, ...), custom_call_target="tpu_custom_call" | custom-call | tf_op jit(solution)/shard_map/james/pallas_call | solution.py:979
  80.4 1.2 %slice_bitcast_fusion = f32[2]{0:T(128)} fusion(f32[8,128]{1,0:T(8,128)} %get-tuple-element.5), kind=kLoop, calls=%fused_computation | loop fusion | bytes 16 | tf_op jit(solution)/shard_map/squeeze | solution.py:990
  81.6 3.1 %copy.18 = f32[32,64,256]{2,1,0:T(8,128)} copy(f32[32,64,256]{2,1,0:T(8,128)} %get-tuple-element.8) | data formatting | bytes 4194304

commit v4 on v3

--- a/solution.py
+++ b/solution.py
@@ -130,7 +130,7 @@
         pl.semaphore_signal(barrier, inc=1, device_id={"gx": lax.rem(ix + d, p.gx)}, device_id_type=MESH)
     for d in range(1, p.gy):
         pl.semaphore_signal(barrier, inc=1, device_id={"gy": lax.rem(iy + d, p.gy)}, device_id_type=MESH)
-    pl.semaphore_wait(barrier, p.gx + p.gy - 2)
+    return barrier
 
 
 def remote(src, dst, send, recv, where):
@@ -155,8 +155,8 @@
 
 
 def edge_sums(p, v_ref, tab_ref, left_ref, right_ref, edge_ref):
-    for t in range(p.n // p.tile):
-        rows = pl.ds(t * p.tile, p.tile)
+    def strip(t, carry):
+        rows = pl.ds(pl.multiple_of(t * p.tile, p.tile), p.tile)
         lam, lsub = tab_ref[0, rows], tab_ref[2, rows]
         left, right = v_ref[0, rows], v_ref[p.sub - 1, rows]
         for i in range(1, p.sub):
@@ -169,6 +169,9 @@
             dev_l = dev_l * lsub + turn(left, -g * p.kb)
             dev_r = dev_r * lsub + turn(right, g * p.kb)
         edge_ref[rows] = jnp.where(p.lanes(p.tile) == 0, dev_l, dev_r)
+        return carry
+
+    lax.fori_loop(0, p.n // p.tile, strip, 0)
 
 
 def line_exchange(p, tab_ref, edge_ref, got_ref, back_ref, ends_ref, sems, between):
@@ -737,10 +740,10 @@
      got_ref, back_ref, ends_ref, got2_ref, back2_ref, ends2_ref,
      dmat_ref, r_ref, g_ref, y_ref, pay_ref, pxs_ref, psum_ref, pys_ref,
      s_ref, coef_ref, c3_ref, e_ref, f_ref,
-     part_ref, xs_ref, sum_ref, ys_ref, fin_ref, z_ref, t_ref, kron_ref, lmode_ref,
+     part_ref, xs_ref, sum_ref, ys_ref, z_ref, t_ref, kron_ref, lmode_ref,
      xg_ref, xgot_ref, yg_ref, ygot_ref, yb_ref, xb_ref, wave_ref,
      table_sems, in_sems, out_sems, land_sems, ghost_out_sems, ghost_land_sems,
-     line_sems, line2_sems, pay_sems, sum_sems, write_sems) = rest[len(names):]
+     line_sems, line2_sems, pay_sems, sum_sems) = rest[len(names):]
     sine_ref, jtab_ref, ktab_ref, wide_ref, lanes_ref, cu_ref, vt_ref, big_ref, gain_ref, same_ref, loc_ref, ltab_ref, rtab_ref, pick_ref = local
     ix, iy = lax.axis_index("gx"), lax.axis_index("gy")
     order = list(range(p.gy // 2, p.gy)) + list(range(1, p.gy // 2))
@@ -757,7 +760,7 @@
             load(c, g).start()
     for copy in staged[1:]:
         copy.start()
-    greet(p)
+    barrier = greet(p)
     staged[0].wait()
 
     def swap(c, d):
@@ -784,16 +787,15 @@
                 part = turn(y[g * block:(g + 1) * block, col * LANES:(col + 1) * LANES], g * p.kb - off)
                 piece = part if piece is None else jnp.where(place == g, part, piece)
             send_ref[q, planes] = piece.reshape(p.step, p.cb, LANES)
-
-        @pl.when(c > 0)
-        def _():
+        if not isinstance(c, int):
             for d in order:
                 swap(c - 1, d).start()
-
         spec_ref[planes, pl.ds(iy * p.cb, p.cb)] = send_ref[iy, planes]
         return carry
 
-    lax.fori_loop(0, p.chunks, transform, 0)
+    transform(0, 0)
+    pl.semaphore_wait(barrier, p.gx + p.gy - 2)
+    lax.fori_loop(1, p.chunks, transform, 0)
     staged[1].wait()
     staged[2].wait()
     mode_tables(p, jtab_ref, ktab_ref, tab_ref)
@@ -915,31 +917,19 @@
             ghost(k, d).wait_recv()
     local_solve(p, xgot_ref, ygot_ref, xb_ref, yb_ref, ltab_ref, lmode_ref, kron_ref, wave_ref, t_ref, z_ref)
 
-    def write(c):
-        rows = pl.ds(c * p.gy, p.gy)
-        return pltpu.make_async_copy(fin_ref.at[rows], out_ref.at[rows], write_sems.at[c])
-
     def finish(c, carry):
         rows = pl.ds(c * p.gy, p.gy)
         y = right_mul(left_mul(kron_ref, z_ref[rows].reshape(p.n, p.n)), sine_ref)
-        fin_ref[rows] = y.reshape(p.gy, p.cb, p.n)
-
-        @pl.when(c > 0)
-        def _():
-            write(c - 1).start()
-
+        out_ref[rows] = y.reshape(p.gy, p.cb, p.n)
         return carry
 
     groups = p.ca // p.gy
-    lax.fori_loop(0, groups, finish, 0)
+    lax.fori_loop(0, groups, finish, 0, unroll=2 if groups % 2 == 0 else 1)
     for c in eb:
         c.wait_recv()
     energy_two = jnp.sum(sum_slots(ys_ref, p.gy))
-    write(groups - 1).start()
     scale = p.h**3 * p.norm
     energy_ref[...] = jnp.where(iota((8, LANES), 1) == 0, energy_one, energy_two) * scale
-    for c in range(groups):
-        write(c).wait()
     for c in ea + eb:
         c.wait_send()
     for d in order:
@@ -959,7 +949,6 @@
     box = (p.gy, p.sub, p.cb, LANES)
     vmem = lambda shape, dtype=f32: pltpu.VMEM(shape, dtype)
     dma = pltpu.SemaphoreType.DMA
-    anywhere = pl.BlockSpec(memory_space=pl.ANY)
     whole = (p.ca, p.cb, p.n)
     scratch = [vmem(t.shape, t.dtype) for t in data]
     scratch += [vmem(whole), vmem(box), vmem(cube), vmem(cube), vmem(cube), vmem((6,) + plane)]
@@ -970,23 +959,23 @@
     scratch += [vmem((3, 2, NBLK, 16, LANES)), vmem((3, NBLK, ROWS, LANES)), vmem((DEG, 5, LANES, LANES), BF16),
                 vmem((DEG, p.n + 4 * p.ca, LANES), BF16), vmem((p.n + 4 * p.ca, p.n))]
     scratch += [vmem((8, LANES)), vmem((p.gx, 8, LANES)), vmem((8, LANES)), vmem((p.gy, 8, LANES)),
-                vmem(whole), vmem(whole), vmem(whole), vmem((2, n, n), BF16), vmem((4, cb, n)),
+                vmem(whole), vmem(whole), vmem((2, n, n), BF16), vmem((4, cb, n)),
                 vmem(plane), vmem((p.gy, cb, LANES)), vmem((p.gy, 2, p.sub, LANES)), vmem((p.gy, 2, p.sub, LANES)),
                 vmem((2, ca, n)), vmem((2, cb, n)), vmem((2, ca, n))]
     most = max(p.gx, p.gy)
     scratch += [dma((len(data),)), dma((p.chunks, p.pack))] + [dma((p.chunks, p.gy))] * 2 + [dma((2, p.gy))] * 2
-    scratch += [dma((4, p.gx))] * 2 + [dma((4, most))] * 2 + [dma((p.ca // p.gy,))]
+    scratch += [dma((4, p.gx))] * 2 + [dma((4, most))] * 2
     potential, energies = pl.pallas_call(
         functools.partial(kernel, p),
-        in_specs=[anywhere] * (1 + len(data)),
-        out_specs=[anywhere, pl.BlockSpec(memory_space=pltpu.VMEM)],
+        in_specs=[pl.BlockSpec(memory_space=pltpu.HBM)] * (1 + len(data)),
+        out_specs=[pl.BlockSpec(memory_space=pltpu.VMEM)] * 2,
         out_shape=[jax.ShapeDtypeStruct(whole, f32), jax.ShapeDtypeStruct((8, LANES), f32)],
         scratch_shapes=scratch,
         compiler_params=pltpu.CompilerParams(
-            collective_id=0, has_side_effects=True, vmem_limit_bytes=56 * 2**20
+            collective_id=0, has_side_effects=True, vmem_limit_bytes=31 * 2**20
         ),
         name="james",
-    )(charge_density, *[jnp.asarray(t) for t in data])
+    )(*[pltpu.with_memory_space_constraint(t, pltpu.HBM) for t in (charge_density, *map(jnp.asarray, data))])
     return potential, energies[0, :2]
 
 

time: 85.3 us -> 79.9 us (0.937)
  Pallas kernels: 79.7 us -> 76.9 us
  local copies, waits for them, and re-layouts: 4.31 us -> 1.83 us
    pallas_call x1, Pallas kernels: 79.7 us -> 76.9 us  [shards(): pl.pallas_call(functools.partial(kernel, p), in_specs=[pl.BlockSpec(memor...]
    unnamed x1, local copies, waits for them, and re-layouts: 3.13 us -> 1.32 us
where the time goes in v4:
time: 79.9 us; the launch traced here: 79.4 us
  Pallas kernels  76.9 us (96%)
  local copies, waits for them, and re-layouts  1.83 us (2%)
    pallas_call x1, Pallas kernels, shards(): pl.pallas_call(functools.partial(kernel, p), in_specs=[pl.BlockSpec(memor...  76.9 us

profile of v4, /device:TPU:1, one launch (start us, length us, event | category | flops | bytes accessed | tf_op | source)
XLA Modules:
  0.0 79.4 jit_solution(6781838033963123686)
XLA Ops:
  0.6 76.9 %james.1 = (f32[32,64,256]{2,1,0:T(8,128)S(1)}, f32[8,128]{1,0:T(8,128)S(1)}) custom-call(f32[32,64,256]{2,1,0:T(8,128)} %rho_ref.1, bf16[2,256,256]{2,1,0:T(8,128)(2,1)} %constant.28.clone.refs_0_, f32[2,256,128]{2,1,0:T(8,128)} %constant.29.clone.refs_1_, f32[4,8,128]{2,1,0:T(8,128)} %constant.30.clone.refs_2_, ...), custom_call_target="tpu_custom_call" | custom-call | tf_op jit(solution)/shard_map/james/pallas_call | solution.py:968
  77.5 0.5 slice_bitcast_fusion
  78.1 1.3 %copy.18 = f32[32,64,256]{2,1,0:T(8,128)} copy(f32[32,64,256]{2,1,0:T(8,128)S(1)} %get-tuple-element.8) | data formatting | bytes 4194304
